TPU v7x, 32 devices: a whole 2x2x4 slice. The times are simulated.
32 devices in a mesh: slides: 2 (over y), seq: 4 (over z), sub: 4 (over x, core).
Axes of the slice: x: 2, y: 2, z: 4, core: 2. Of those that a mesh axis runs over, the one named last changes fastest.
Arguments:
- q_heads: bfloat16 [8192, 768], P(('slides', 'seq'), 'sub'), parts along dimension 0, may hold values from -8 to 8
- k_heads: bfloat16 [8192, 768], P(('slides', 'seq'), 'sub'), parts along dimension 0, may hold values from -8 to 8
- v_heads: bfloat16 [8192, 768], P(('slides', 'seq'), 'sub'), parts along dimension 0, may hold values from -6 to 6
- w_out: bfloat16 [768, 768], replicated, may hold values from -0.21875 to 0.21875
- offsets: int32 [2, 16], replicated, may hold values from 0 to 15, as said below
- valid: int32 [2], P('slides'), parts along dimension 0, may hold values from 3073 to 4096
Outputs:
- mixed: bfloat16 [8192, 768], P(('slides', 'seq'), 'sub'), parts along dimension 0
There are 2 independent parts, one for each index of `slides`. A program takes and returns all parts, laid end to end along the dimension named above; an argument that names none is the same for every part. Nothing has to cross between parts.
Inputs may be any that keep to these rules, and one draw needn't show every extreme that they name: `offsets`: row 0 lies below 4, row 1 below 16. Tiles at positions valid[0] and beyond are padding.
All inputs are finite; a program needn't handle non-finite values.
Results may differ from a plain program's by a relative error of at most 0.012.
Values may be sent and summed in bfloat16 or wider, within the bound.
A program may use at most 64 MiB of HBM per device.

v0:
```python
import jax
import jax.numpy as jnp
from jax import lax
from jax.sharding import PartitionSpec as P

HS = 48
GROUP = 4
R1 = 4
R2 = 16


NEG_FILL = -1e30


def swapped(value, axis, stride):
    mask = 2**stride
    pairs = [(source, source ^ mask) for source in range(lax.axis_size(axis))]
    return lax.ppermute(value, axis, pairs)


def pick_rows(source, stride, chosen):
    grouped = source.reshape(source.shape[0] // stride, stride, source.shape[1], source.shape[2])
    onehot = jnp.arange(stride, dtype=jnp.int32)[:, None] == chosen[None, :]
    return jnp.sum(
        jnp.where(onehot[None, :, :, None], grouped, jnp.zeros((), source.dtype)), axis=1
    )


def spread_back(maxima, totals, numer, stride, chosen):
    onehot = (jnp.arange(stride, dtype=jnp.int32)[:, None] == chosen[None, :])[None]
    count = maxima.shape[0] * stride
    full_max = jnp.where(onehot, maxima[:, None, :], NEG_FILL).reshape(count, maxima.shape[1])
    full_tot = jnp.where(onehot, totals[:, None, :], 0.0).reshape(count, maxima.shape[1])
    full_num = jnp.where(onehot[..., None], numer[:, None, :, :], 0.0).reshape(
        count, numer.shape[1], numer.shape[2]
    )
    return (full_max, full_tot, full_num)


def block_stats(q_sel, k_sel, v_sel, live):
    n_query = q_sel.shape[0]
    width = min(512, n_query)
    live_rows = live.T[:, None, :]

    def attend(q_blk):
        scores = jnp.einsum(
            "qhd,khd->hqk", q_blk, k_sel, preferred_element_type=jnp.float32
        ) * HS ** (-0.5)
        scores = jnp.where(live_rows, scores, NEG_FILL)
        peak = jnp.max(scores, axis=2)
        probs = jnp.exp(scores - peak[:, :, None])
        mass = jnp.sum(probs, axis=2)
        weighted = jnp.einsum(
            "hqk,khd->qhd", probs.astype(jnp.bfloat16), v_sel, preferred_element_type=jnp.float32
        )
        return (peak.T, mass.T, weighted)

    peak, mass, weighted = lax.map(
        attend, q_sel.reshape(n_query // width, width, q_sel.shape[1], q_sel.shape[2])
    )
    return (
        peak.reshape(n_query, q_sel.shape[1]),
        mass.reshape(n_query, q_sel.shape[1]),
        weighted.reshape(n_query, q_sel.shape[1], q_sel.shape[2]),
    )


def local(q_heads, k_heads, v_heads, w_out, offsets, valid):
    tok_rows = q_heads.shape[0]
    head_cols = q_heads.shape[1]
    local_heads = head_cols // HS
    seq_index = lax.axis_index("seq")
    sub_index = lax.axis_index("sub")
    block_start = seq_index * tok_rows
    mine = lax.dynamic_slice_in_dim(offsets, sub_index * local_heads, local_heads, 1)
    limit = valid[0]
    queries = q_heads.reshape(tok_rows, local_heads, HS)
    keys_local = k_heads.reshape(tok_rows, local_heads, HS)
    values_local = v_heads.reshape(tok_rows, local_heads, HS)
    own_rows = jnp.arange(tok_rows, dtype=jnp.int32)
    live_near = jnp.broadcast_to((block_start + own_rows < limit)[:, None], (tok_rows, local_heads))
    near = block_stats(queries, keys_local, values_local, live_near)
    middle_offs = mine[0]
    middle_rows = tok_rows // R1
    q_middle = pick_rows(queries, R1, middle_offs)
    kv_middle = jnp.concatenate(
        [
            pick_rows(keys_local, R1, middle_offs).reshape(middle_rows, head_cols),
            pick_rows(values_local, R1, middle_offs).reshape(middle_rows, head_cols),
        ],
        axis=1,
    )
    block_ids = seq_index.reshape(1)
    for bit_index in range(GROUP.bit_length() - 1):
        partner = swapped(kv_middle, "seq", bit_index)
        kv_middle = jnp.concatenate([kv_middle, partner], axis=0)
        block_ids = jnp.concatenate([block_ids, block_ids ^ 1 << bit_index])
    middle_pos = (
        block_ids[:, None] * tok_rows + jnp.arange(middle_rows, dtype=jnp.int32)[None, :] * R1
    )
    live_middle = middle_pos.reshape(-1, 1) + middle_offs[None, :] < limit
    middle_count = kv_middle.shape[0]
    middle = block_stats(
        q_middle,
        kv_middle[:, :head_cols].reshape(middle_count, local_heads, HS),
        kv_middle[:, head_cols:].reshape(middle_count, local_heads, HS),
        live_middle,
    )
    middle = spread_back(middle[0], middle[1], middle[2], R1, middle_offs)
    wide_offs = mine[1]
    wide_rows = tok_rows // R2
    q_wide = pick_rows(queries, R2, wide_offs)
    kv_wide = jnp.concatenate(
        [
            pick_rows(keys_local, R2, wide_offs).reshape(wide_rows, head_cols),
            pick_rows(values_local, R2, wide_offs).reshape(wide_rows, head_cols),
        ],
        axis=1,
    )
    piece = lax.all_gather(kv_wide, "seq", axis=0, tiled=True)
    run_peak = jnp.full((wide_rows, local_heads), NEG_FILL, jnp.float32)
    piece_len = piece.shape[0]
    global_row = jnp.arange(piece_len, dtype=jnp.int32)
    position = global_row // wide_rows * tok_rows + global_row % wide_rows * R2
    live_piece = position[:, None] + wide_offs[None, :] < limit
    piece_peak, piece_mass, piece_num = block_stats(
        q_wide,
        piece[:, :head_cols].reshape(piece_len, local_heads, HS),
        piece[:, head_cols:].reshape(piece_len, local_heads, HS),
        live_piece,
    )
    new_peak = jnp.maximum(run_peak, piece_peak)
    new_scale = jnp.exp(piece_peak - new_peak)
    wide = (new_peak, new_scale * piece_mass, new_scale[..., None] * piece_num)
    wide = spread_back(wide[0], wide[1], wide[2], R2, wide_offs)
    top = jnp.maximum(jnp.maximum(near[0], middle[0]), wide[0])
    denom = jnp.zeros_like(top)
    numer = jnp.zeros_like(near[2])
    for peak, mass, partial_num in (near, middle, wide):
        weight = jnp.exp(peak - top)
        denom = denom + weight * mass
        numer = numer + weight[..., None] * partial_num
    attn = (numer / denom[..., None]).reshape(tok_rows, head_cols).astype(jnp.bfloat16)
    w_cols = lax.dynamic_slice_in_dim(w_out, sub_index * head_cols, head_cols, 1)
    projected = jnp.dot(
        lax.all_gather(attn, "sub", axis=1, tiled=True), w_cols, preferred_element_type=jnp.float32
    )
    keep = block_start + own_rows < limit
    return jnp.where(keep[:, None], projected, 0.0).astype(jnp.bfloat16)


def solution(mesh):
    placed = (
        P(("slides", "seq"), "sub"),
        P(("slides", "seq"), "sub"),
        P(("slides", "seq"), "sub"),
        P(),
        P(),
        P("slides"),
    )
    return jax.shard_map(
        local, mesh=mesh, in_specs=placed, out_specs=P(("slides", "seq"), "sub"), check_vma=False
    )
```

profile of v0, /device:TPU:1, one launch (start us, length us, event | category | flops | bytes accessed | tf_op | source)
XLA Modules:
  0.0 160.2 jit_solution(14482707209866753938)
XLA Ops:
  6.5 1.3 copy.46
  8.6 1.2 copy.47
  9.8 1.2 copy.49
  11.0 1.5 reshape_reshape.22
  12.5 1.5 reshape_reshape.23
  14.1 1.5 reshape_reshape.24
  15.6 6.2 %select_reduce_fusion.5 = (bf16[256,4,48]{2,1,0:T(4,128)(2,1)}, bf16[256,4,48]{2,1,0:T(4,128)(2,1)}, bf16[256,4,48]{2,1,0:T(4,128)(2,1)}) fusion(bf16[256,4,4,48]{3,2,1,0:T(4,128)(2,1)} %reshape_reshape.22, pred[4,4]{1,0:T(4,128)(4,1)S(1)} %iota_compare_fusion.1, bf16[256,4,4,48]{3,2,1,0:T(4,128)(2,1)} %reshape_reshape.23, ...), kind=kLoop, calls=%fused_computation.36 | loop fusion | flops 1032192 | bytes 1474576 | tf_op jit(solution)/shard_map/reduce_sum | solution.py:24
  21.8 1.8 %copy.50 = bf16[256,4,48]{0,2,1:T(8,128)(2,1)} copy(bf16[256,4,48]{2,1,0:T(4,128)(2,1)} %get-tuple-element.148) | data formatting | bytes 196608 | tf_op jit(solution)/shard_map/reduce_sum | solution.py:24
  23.6 1.7 %copy.48 = bf16[256,4,48]{0,2,1:T(8,128)(2,1)} copy(bf16[256,4,48]{2,1,0:T(4,128)(2,1)} %get-tuple-element.147) | data formatting | bytes 196608 | tf_op jit(solution)/shard_map/reduce_sum | solution.py:24
  25.4 1.6 %pad_maximum_fusion.2 = bf16[256,384]{0,1:T(8,128)(2,1)} fusion(bf16[256,192]{0,1:T(8,128)(2,1)} %bitcast.123, bf16[256,192]{0,1:T(8,128)(2,1)} %bitcast.126), kind=kLoop, calls=%fused_computation.52 | loop fusion | flops 393216 | bytes 393216 | tf_op jit(solution)/shard_map/concatenate | solution.py:86
  27.0 2.1 %collective-permute-start = (bf16[256,384]{0,1:T(8,128)(2,1)}, bf16[256,384]{0,1:T(8,128)(2,1)}, u32[]{:S(2)}, u32[]{:S(2)}) collective-permute-start(bf16[256,384]{0,1:T(8,128)(2,1)} %pad_maximum_fusion.2), channel_id=1, source_target_pairs={{0,4},{4,0},{8,12},{12,8},{1,5},{5,1},{9,13},{13,9},{2,6},{6,2},{1... | collective-permute-start | bytes 589832 | tf_op jit(solution)/shard_map/ppermute | solution.py:18
  29.1 1.0 reshape_reshape.21
  30.1 1.5 reshape_reshape.25
  31.6 1.5 reshape_reshape.26
  33.2 1.5 reshape_reshape.27
  35.6 28.2 %while.3 = (s32[]{:T(128)}, f32[2,512,4]{1,2,0:T(4,128)}, f32[2,512,4]{1,2,0:T(4,128)}, f32[2,512,4,48]{1,0,3,2:T(2,128)}, bf16[2,512,4,48]{1,3,2,0:T(8,128)(2,1...) while((s32[]{:T(128)}, f32[2,512,4]{1,2,0:T(4,128)}, ...), condition=%wide.region_3.4_spmd.clone, body=%wide.region_0.3_spmd.clone.sunk | while | flops 425717760 | bytes 30018820 | solution.py:58
  35.8 1.5 fusion.68
  37.3 2.1 %fusion.69 = f32[4,512]{1,0:T(4,128)S(1)} fusion(f32[4,512,1024]{2,1,0:T(8,128)S(1)} %get-tuple-element.239, f32[4,512]{1,0:T(4,128)S(1)} %get-tuple-element.240, pred[1024]{0:T(1024)(128)(4,1)S(1)} %get-tuple-element.270), kind=kLoop, calls=%fused_computation.5.clone.1 | loop fusion | flops 8386560 | bytes 8406016 | tf_op jit(solution)/shard_map/while/body/eval_jaxpr/reduce_sum | solution.py:52
  39.4 1.8 %fusion.70 = f32[1,512,4,48]{1,3,2,0:T(8,128)S(1)} fusion(bf16[1024,4,48]{0,2,1:T(8,128)(2,1)S(1)} %copy-done.10, f32[4,512,1024]{2,1,0:T(8,128)S(1)} %get-tuple-element.239, f32[4,512]{1,0:T(4,128)S(1)} %get-tuple-element.240, pred[1024]{0:T(1024)(128)(4,1)S(1)} %get-tuple-element.270), kind=kOutput, calls=%fused_computation.8.clone.1 | convolution fusion | flops 209715200 | bytes 9184256 | tf_op jit(solution)/shard_map/while/body/eval_jaxpr/hqk,khd->qhd/dot_general | solution.py:53
  41.7 8.1 %dynamic_update_slice.35 = f32[2,512,4,48]{1,0,3,2:T(2,128)} dynamic-update-slice(f32[2,512,4,48]{1,0,3,2:T(2,128)} %get-tuple-element.256, f32[1,512,4,48]{1,0,3,2:T(1,128)S(1)} %copy.83, s32[]{:T(128)S(6)} %copy.91, s32[]{:T(128)} %constant.119.clone.1..sunk, s32[]{:T(128)} %constant.119.clone.1..sunk, s32[]{:T(128)} %constant.119.clone.1..sunk) | dynamic-update-slice | bytes 786436 | tf_op jit(solution)/shard_map/while/body/jit(dynamic_update_index_in_dim)/dynamic_update_slice | solution.py:58
  49.8 1.5 fusion.68
  51.3 2.1 %fusion.69 = f32[4,512]{1,0:T(4,128)S(1)} fusion(f32[4,512,1024]{2,1,0:T(8,128)S(1)} %get-tuple-element.239, f32[4,512]{1,0:T(4,128)S(1)} %get-tuple-element.240, pred[1024]{0:T(1024)(128)(4,1)S(1)} %get-tuple-element.270), kind=kLoop, calls=%fused_computation.5.clone.1 | loop fusion | flops 8386560 | bytes 8406016 | tf_op jit(solution)/shard_map/while/body/eval_jaxpr/reduce_sum | solution.py:52
  53.4 1.8 %fusion.70 = f32[1,512,4,48]{1,3,2,0:T(8,128)S(1)} fusion(bf16[1024,4,48]{0,2,1:T(8,128)(2,1)S(1)} %copy-done.10, f32[4,512,1024]{2,1,0:T(8,128)S(1)} %get-tuple-element.239, f32[4,512]{1,0:T(4,128)S(1)} %get-tuple-element.240, pred[1024]{0:T(1024)(128)(4,1)S(1)} %get-tuple-element.270), kind=kOutput, calls=%fused_computation.8.clone.1 | convolution fusion | flops 209715200 | bytes 9184256 | tf_op jit(solution)/shard_map/while/body/eval_jaxpr/hqk,khd->qhd/dot_general | solution.py:53
  55.7 8.1 %dynamic_update_slice.35 = f32[2,512,4,48]{1,0,3,2:T(2,128)} dynamic-update-slice(f32[2,512,4,48]{1,0,3,2:T(2,128)} %get-tuple-element.256, f32[1,512,4,48]{1,0,3,2:T(1,128)S(1)} %copy.83, s32[]{:T(128)S(6)} %copy.91, s32[]{:T(128)} %constant.119.clone.1..sunk, s32[]{:T(128)} %constant.119.clone.1..sunk, s32[]{:T(128)} %constant.119.clone.1..sunk) | dynamic-update-slice | bytes 786436 | tf_op jit(solution)/shard_map/while/body/jit(dynamic_update_index_in_dim)/dynamic_update_slice | solution.py:58
  63.8 2.2 %copy.73 = f32[24,8,2,512]{3,1,2,0:T(8,128)} copy(f32[24,8,2,512]{3,2,1,0:T(2,128)} %bitcast.129) | data formatting | bytes 1572864
  66.0 4.9 %select_reduce_fusion.2 = (bf16[64,4,48]{2,1,0:T(4,128)(2,1)S(1)}, bf16[64,4,48]{2,1,0:T(4,128)(2,1)S(1)}, bf16[64,4,48]{2,1,0:T(4,128)(2,1)S(1)}) fusion(bf16[64,16,4,48]{3,2,1,0:T(4,128)(2,1)S(1)} %copy-done.2, pred[16,4]{1,0:T(8,128)(4,1)S(1)} %iota_compare_fusion, bf16[64,16,4,48]{3,2,1,0:T(4,128)(2,1)} %reshape_reshape.26, ...), kind=kLoop, calls=%fused_computation.33 | loop fusion | flops 1142784 | bytes 1253440 | tf_op jit(solution)/shard_map/reduce_sum | solution.py:24
  71.3 11.8 %all_gather.6 = bf16[256,384]{1,0:T(8,128)(2,1)S(1)} all-gather(bf16[64,384]{1,0:T(8,128)(2,1)S(1)} %copy.58), channel_id=1, replica_groups=mesh['slides'=2,'seq'=4,'sub'=4] {'seq'}, dimensions={0}, use_global_device_ids=true | all-gather | bytes 245760 | tf_op jit(solution)/shard_map/all_gather | solution.py:120
  85.0 1.2 broadcast_in_dim.317
  86.2 1.9 %broadcast_in_dim.318 = f32[1024,192]{1,0:T(8,128)} reshape(f32[64,16,4,48]{3,2,1,0:T(4,128)S(1)} %broadcast_in_dim.317) | data formatting | bytes 1572864 | tf_op jit(solution)/shard_map/jit(_where)/broadcast_in_dim | solution.py:34
  88.1 2.5 %copy.66 = f32[1024,192]{0,1:T(8,128)} copy(f32[1024,192]{1,0:T(8,128)} %broadcast_in_dim.318) | data formatting | bytes 1572864 | tf_op jit(solution)/shard_map/jit(_where)/broadcast_in_dim | solution.py:34
  90.8 1.0 pad_maximum_fusion.1
  94.5 16.7 %collective-permute-done.1 = bf16[512,384]{0,1:T(8,128)(2,1)S(1)} collective-permute-done((bf16[512,384]{0,1:T(8,128)(2,1)S(1)}, bf16[512,384]{0,1:T(8,128)(2,1)S(1)}, u32[]{:S(2)}, u32[]{:S(2)}) %collective-permute-start.1) | collective-permute-done | bytes 393248 | tf_op jit(solution)/shard_map/ppermute | solution.py:18
  111.2 1.0 pad_maximum_fusion
  112.3 0.8 fusion.17
  113.1 1.7 %fusion.18 = f32[4,256]{1,0:T(4,128)} fusion(f32[4,256,1024]{2,1,0:T(8,128)S(1)} %get-tuple-element.185, f32[4,256]{1,0:T(4,128)S(1)} %get-tuple-element.184, pred[4,1024]{1,0:T(4,128)(4,1)S(1)} %add_compare_fusion), kind=kLoop, calls=%fused_computation.20 | loop fusion | flops 4193280 | bytes 4206592 | tf_op jit(solution)/shard_map/while/body/eval_jaxpr/reduce_sum | solution.py:52
  114.8 1.2 fusion.25
  116.0 1.0 copy.62
  117.0 1.3 broadcast_in_dim.312
  118.3 1.9 %broadcast_in_dim.313 = f32[1024,192]{1,0:T(8,128)} reshape(f32[256,4,4,48]{3,2,1,0:T(4,128)S(1)} %broadcast_in_dim.312) | data formatting | bytes 1572864 | tf_op jit(solution)/shard_map/jit(_where)/broadcast_in_dim | solution.py:34
  120.2 1.7 %copy.63 = f32[1024,192]{0,1:T(8,128)S(1)} copy(f32[1024,192]{1,0:T(8,128)} %broadcast_in_dim.313) | data formatting | bytes 1572864 | tf_op jit(solution)/shard_map/jit(_where)/broadcast_in_dim | solution.py:34
  121.9 1.7 %broadcast_in_dim.319 = f32[256,4,4]{1,0,2:T(8,128)} broadcast(f32[256,4]{0,1:T(4,128)} %bitcast.137), dimensions={0,2} | broadcast | bytes 20480 | tf_op jit(solution)/shard_map/jit(_where)/broadcast_in_dim | solution.py:33
  123.5 1.9 %broadcast_in_dim.320 = f32[1024,4]{0,1:T(4,128)} reshape(f32[256,4,4]{1,0,2:T(8,128)} %broadcast_in_dim.319) | data formatting | bytes 32768 | tf_op jit(solution)/shard_map/jit(_where)/broadcast_in_dim | solution.py:33
  125.4 1.0 broadcast_in_dim.298
  126.4 1.9 %broadcast_in_dim.299 = f32[1024,4]{0,1:T(4,128)} reshape(f32[256,4,4]{1,0,2:T(8,128)} %broadcast_in_dim.298) | data formatting | bytes 32768 | tf_op jit(solution)/shard_map/jit(_where)/broadcast_in_dim | solution.py:32
  128.4 0.8 multiply_add_fusion
  129.2 1.1 fusion.29
  130.3 20.2 %all-gather.2.cloned.1.call-done = bf16[1024,768]{0,1:T(8,128)(2,1)} async-done(((bf16[1024,192]{0,1:T(8,128)(2,1)}), bf16[1024,768]{0,1:T(8,128)(2,1)}) %all-gather.2.cloned.1.call-update) | async-done | bytes 1572880 | tf_op jit(solution)/shard_map/all_gather | solution.py:146
  150.5 2.9 %fusion.23 = bf16[1024,192]{0,1:T(8,128)(2,1)} fusion(bf16[1024,768]{0,1:T(8,128)(2,1)} %all-gather.2.cloned.1.call-done, bf16[768,768]{1,0:T(8,128)(2,1)S(1)} %copy-done, s32[]{:T(128)S(6)} %select_n.145, pred[1024]{0:T(1024)(128)(4,1)S(1)} %get-tuple-element.278), kind=kOutput, calls=%fused_computation.25 | convolution fusion | flops 302383104 | bytes 2360324 | tf_op jit(solution)/shard_map/dot_general | solution.py:145
  (96 shorter events, 7.1 us)
Async XLA Ops:
  6.5 144.0 %copy-start = (bf16[768,768]{1,0:T(8,128)(2,1)S(1)}, bf16[768,768]{1,0:T(8,128)(2,1)}, u32[]{:S(2)}) copy-start(bf16[768,768]{1,0:T(8,128)(2,1)} %param.11) | copy-start | bytes 3538948
  6.5 144.0 %all-gather.2.cloned.1.call-start = ((), (), s32[]{:S(2)}) async-start(), calls=%async_computation | async-start | bytes 1966080 | tf_op jit(solution)/shard_map/all_gather | solution.py:146
  8.6 13.2 %copy-start.15 = (s32[4]{0:T(128)}, s32[4]{0:T(128)S(1)}, u32[]{:S(2)}) copy-start(s32[4]{0:T(128)S(1)} %get-tuple-element.180) | copy-start | bytes 52
  12.5 16.6 %copy-start.5 = (bf16[1024,192]{0,1:T(8,128)(2,1)S(1)}, bf16[1024,192]{0,1:T(8,128)(2,1)}, u32[]{:S(2)}) copy-start(bf16[1024,192]{0,1:T(8,128)(2,1)} %param.8) | copy-start | bytes 1179652
  12.5 3.1 %copy-start.17 = (pred[4,4]{1,0:T(4,128)(4,1)}, pred[4,4]{1,0:T(4,128)(4,1)S(1)}, u32[]{:S(2)}) copy-start(pred[4,4]{1,0:T(4,128)(4,1)S(1)} %iota_compare_fusion.1) | copy-start | bytes 52
  21.8 13.7 %copy-start.1 = (bf16[1024,192]{0,1:T(8,128)(2,1)S(1)}, bf16[1024,192]{0,1:T(8,128)(2,1)}, u32[]{:S(2)}) copy-start(bf16[1024,192]{0,1:T(8,128)(2,1)} %param.9) | copy-start | bytes 1179652
  21.8 12.9 %copy-start.18 = (pred[4,4]{1,0:T(4,128)(4,1)S(1)}, pred[4,4]{1,0:T(4,128)(4,1)}, u32[]{:S(2)}) copy-start(pred[4,4]{1,0:T(4,128)(4,1)} %copy-done.17) | copy-start | bytes 52
  27.0 63.8 %collective-permute-start = (bf16[256,384]{0,1:T(8,128)(2,1)}, bf16[256,384]{0,1:T(8,128)(2,1)}, u32[]{:S(2)}, u32[]{:S(2)}) collective-permute-start(bf16[256,384]{0,1:T(8,128)(2,1)} %pad_maximum_fusion.2), channel_id=1, source_target_pairs={{0,4},{4,0},{8,12},{12,8},{1,5},{5,1},{9,13},{13,9},{2,6},{6,2},{1... | collective-permute-start | bytes 589832 | tf_op jit(solution)/shard_map/ppermute | solution.py:18
  30.1 4.7 %copy-start.6 = (bf16[2,512,4,48]{1,0,3,2:T(2,128)(2,1)S(1)}, bf16[2,512,4,48]{1,0,3,2:T(2,128)(2,1)}, u32[]{:S(2)}) copy-start(bf16[2,512,4,48]{1,0,3,2:T(2,128)(2,1)} %reshape_reshape.21) | copy-start | bytes 1179652
  35.5 30.5 %copy-start.2 = (bf16[64,16,4,48]{3,2,1,0:T(4,128)(2,1)S(1)}, bf16[64,16,4,48]{3,2,1,0:T(4,128)(2,1)}, u32[]{:S(2)}) copy-start(bf16[64,16,4,48]{3,2,1,0:T(4,128)(2,1)} %reshape_reshape.25) | copy-start | bytes 1179652
  37.2 2.1 %copy-start.11 = (f32[2,512,4]{1,2,0:T(4,128)S(1)}, f32[2,512,4]{1,2,0:T(4,128)}, u32[]{:S(2)}) copy-start(f32[2,512,4]{1,2,0:T(4,128)} %get-tuple-element.254) | copy-start | bytes 49156 | tf_op jit(solution)/shard_map/while
  37.2 2.1 %copy-start.13 = (f32[2,512,4]{1,2,0:T(4,128)S(1)}, f32[2,512,4]{1,2,0:T(4,128)}, u32[]{:S(2)}) copy-start(f32[2,512,4]{1,2,0:T(4,128)} %get-tuple-element.255) | copy-start | bytes 49156 | tf_op jit(solution)/shard_map/while
  37.3 2.2 %copy-start.10 = (bf16[1024,4,48]{0,2,1:T(8,128)(2,1)S(1)}, bf16[1024,4,48]{0,2,1:T(8,128)(2,1)}, u32[]{:S(2)}) copy-start(bf16[1024,4,48]{0,2,1:T(8,128)(2,1)} %get-tuple-element.269) | copy-start | bytes 1179652 | tf_op jit(solution)/shard_map/while
  39.4 1.9 %copy-start.12 = (f32[2,512,4]{1,2,0:T(4,128)}, f32[2,512,4]{1,2,0:T(4,128)S(1)}, u32[]{:S(2)}) copy-start(f32[2,512,4]{1,2,0:T(4,128)S(1)} %get-tuple-element.264) | copy-start | bytes 49156 | tf_op jit(solution)/shard_map/while
  39.4 1.9 %copy-start.14 = (f32[2,512,4]{1,2,0:T(4,128)}, f32[2,512,4]{1,2,0:T(4,128)S(1)}, u32[]{:S(2)}) copy-start(f32[2,512,4]{1,2,0:T(4,128)S(1)} %get-tuple-element.265) | copy-start | bytes 49156 | tf_op jit(solution)/shard_map/while
  51.2 2.1 %copy-start.11 = (f32[2,512,4]{1,2,0:T(4,128)S(1)}, f32[2,512,4]{1,2,0:T(4,128)}, u32[]{:S(2)}) copy-start(f32[2,512,4]{1,2,0:T(4,128)} %get-tuple-element.254) | copy-start | bytes 49156 | tf_op jit(solution)/shard_map/while
  51.3 2.1 %copy-start.13 = (f32[2,512,4]{1,2,0:T(4,128)S(1)}, f32[2,512,4]{1,2,0:T(4,128)}, u32[]{:S(2)}) copy-start(f32[2,512,4]{1,2,0:T(4,128)} %get-tuple-element.255) | copy-start | bytes 49156 | tf_op jit(solution)/shard_map/while
  51.3 2.2 %copy-start.10 = (bf16[1024,4,48]{0,2,1:T(8,128)(2,1)S(1)}, bf16[1024,4,48]{0,2,1:T(8,128)(2,1)}, u32[]{:S(2)}) copy-start(bf16[1024,4,48]{0,2,1:T(8,128)(2,1)} %get-tuple-element.269) | copy-start | bytes 1179652 | tf_op jit(solution)/shard_map/while
  53.4 1.9 %copy-start.12 = (f32[2,512,4]{1,2,0:T(4,128)}, f32[2,512,4]{1,2,0:T(4,128)S(1)}, u32[]{:S(2)}) copy-start(f32[2,512,4]{1,2,0:T(4,128)S(1)} %get-tuple-element.264) | copy-start | bytes 49156 | tf_op jit(solution)/shard_map/while
  53.4 1.9 %copy-start.14 = (f32[2,512,4]{1,2,0:T(4,128)}, f32[2,512,4]{1,2,0:T(4,128)S(1)}, u32[]{:S(2)}) copy-start(f32[2,512,4]{1,2,0:T(4,128)S(1)} %get-tuple-element.265) | copy-start | bytes 49156 | tf_op jit(solution)/shard_map/while
  83.8 7.0 %copy-start.7 = (bf16[256,4,48]{0,2,1:T(8,128)(2,1)S(1)}, bf16[256,4,48]{0,2,1:T(8,128)(2,1)}, u32[]{:S(2)}) copy-start(bf16[256,4,48]{0,2,1:T(8,128)(2,1)} %copy.50) | copy-start | bytes 294916
  83.8 7.0 %copy-start.8 = (bf16[256,4,48]{0,2,1:T(8,128)(2,1)S(1)}, bf16[256,4,48]{0,2,1:T(8,128)(2,1)}, u32[]{:S(2)}) copy-start(bf16[256,4,48]{0,2,1:T(8,128)(2,1)} %copy.48) | copy-start | bytes 294916
  85.0 9.4 %copy-start.16 = (s32[4]{0:T(128)S(1)}, s32[4]{0:T(128)}, u32[]{:S(2)}) copy-start(s32[4]{0:T(128)} %copy-done.15) | copy-start | bytes 52
  88.1 24.2 %copy-start.9 = (bf16[256,4,48]{2,1,0:T(4,128)(2,1)S(1)}, bf16[256,4,48]{2,1,0:T(4,128)(2,1)}, u32[]{:S(2)}) copy-start(bf16[256,4,48]{2,1,0:T(4,128)(2,1)} %get-tuple-element.146) | copy-start | bytes 294916
  91.7 19.5 %collective-permute-start.1 = (bf16[512,384]{0,1:T(8,128)(2,1)S(1)}, bf16[512,384]{0,1:T(8,128)(2,1)S(1)}, u32[]{:S(2)}, u32[]{:S(2)}) collective-permute-start(bf16[512,384]{0,1:T(8,128)(2,1)S(1)} %pad_maximum_fusion.1), channel_id=1, source_target_pairs={{0,8},{4,12},{8,0},{12,4},{1,9},{5,13},{9,1},{13,5},{2,10},{6,14},... | collective-permute-start | bytes 1179656 | tf_op jit(solution)/shard_map/ppermute | solution.py:18
  120.2 9.0 %copy-start.3 = (f32[1024,192]{0,1:T(8,128)S(1)}, f32[1024,192]{0,1:T(8,128)}, u32[]{:S(2)}) copy-start(f32[1024,192]{0,1:T(8,128)} %copy.66) | copy-start | bytes 2359300
  120.2 9.0 %copy-start.4 = (f32[24,8,2,512]{3,1,2,0:T(8,128)S(1)}, f32[24,8,2,512]{3,1,2,0:T(8,128)}, u32[]{:S(2)}) copy-start(f32[24,8,2,512]{3,1,2,0:T(8,128)} %copy.73) | copy-start | bytes 2359300
Sparse Core Ops, SparseCore 0:
  130.4 20.0 all-gather.1
where the time goes:
time: 162 us; the launch traced here: 160 us
  local copies, waits for them, and re-layouts  59.1 us (36%)
  waiting for transfers between devices  36.9 us (23%)
  other arithmetic  23.1 us (14%)
  between operations  14.3 us (9%)
  matrix products  12 us (7%)
  blocking collectives  11.8 us (7%)
  starting transfers between devices  2.59 us (2%)
    all_gather x1, waiting for transfers between devices, local(): lax.all_gather(attn, 'sub', axis=1, tiled=True)  20.2 us
    dynamic_update_slice x6, local copies, waits for them, and re-layouts, block_stats(): lax.map(attend, q_sel.reshape(n_query // width, width, q_sel.shape[1], q_...  17 us
    ppermute x2, waiting for transfers between devices, swapped(): return lax.ppermute(value, axis, pairs)  16.7 us
    all_gather x1, blocking collectives, local(): piece = lax.all_gather(kv_wide, 'seq', axis=0, tiled=True)  11.8 us
    reduce_sum x2, other arithmetic, pick_rows(): jnp.sum(jnp.where(onehot[None, :, :, None], grouped, jnp.zeros((), source...  11.1 us
    broadcast_in_dim x6, local copies, waits for them, and re-layouts, spread_back(): jnp.where(onehot[..., None], numer[:, None, :, :], 0.0)  10.4 us
    another operation x6, local copies, waits for them, and re-layouts, pick_rows(): source.reshape(source.shape[0] // stride, stride, source.shape[1], source...  9.14 us
    reduce_sum x4, other arithmetic, attend(): mass = jnp.sum(probs, axis=2)  6.02 us
  transfers between devices with their start and end apart: 3, of which 2 were waited for; matrix products, arithmetic and copies ran while one was open for 32% of the time, Pallas kernels for 0%

commit v1 on v0

v1 whole, which is shorter than its diff:
```python
import functools

import jax
import jax.numpy as jnp
from jax import lax
from jax.experimental import pallas as pl
from jax.experimental.pallas import tpu as pltpu
from jax.sharding import PartitionSpec as P

HS = 48
GROUP = 4
R1 = 4
R2 = 16
LANES = 128
HALF = 64
MASKED = -1e30
MESH = pl.DeviceIdType.MESH
EXP_SCALE = HS ** (-0.5) * 1.4426950408889634


def pick(masks, parts):
    out = parts[-1]
    for mask, part in zip(masks[:-1], parts[:-1]):
        out = jnp.where(mask, part, out)
    return out


def kernel(
    n_seq, n_sub, heads,
    q_ref, k_ref, v_ref, w_ref, off_ref, valid_ref, o_ref,
    sq, sk, sv, qp, kx, vx, qm, qw, wide, mid, wk, wv, mk, mv,
    st_m, st_l, st_a, xg, wl, wr, so,
    wide_send, wide_recv, mid_send, mid_recv, x_send, x_recv,
):
    rows = q_ref.shape[0]
    cols = heads * HS
    phase = rows // R1
    strip = rows // R2
    subs = R2 // R1
    half_rows = phase // 2
    seq = lax.axis_index("seq")
    sub = lax.axis_index("sub")
    pos = lax.rem(seq, GROUP)
    group0 = seq - pos
    limit = valid_ref[0]
    has_left = pos > 0
    has_right = pos < GROUP - 1
    bits = [1 << b for b in reversed(range(n_sub.bit_length() - 1))]

    barrier = pltpu.get_barrier_semaphore()
    for step in range(1, n_seq):
        pl.semaphore_signal(
            barrier, inc=1, device_id={"seq": lax.rem(seq + step, n_seq)}, device_id_type=MESH
        )
    for bit in bits:
        pl.semaphore_signal(barrier, inc=1, device_id={"sub": sub ^ bit}, device_id_type=MESH)

    lane = lax.broadcasted_iota(jnp.int32, (1, LANES), 1)
    low = lane < HALF

    def off_lanes(which, first_head, base, tile):
        at = lane + tile * LANES - base
        out = jnp.zeros((1, LANES), jnp.int32)
        for h in range(heads):
            here = ((at >= h * HS) & (at < (h + 1) * HS)) | (at == cols + h)
            out = jnp.where(here, off_ref[which, first_head + h], out)
        return out

    def head_mask(h, base, tiles=2):
        at = lax.broadcasted_iota(jnp.int32, (1, tiles * LANES), 1) - base
        here = (at >= h * HS) & (at < (h + 1) * HS)
        if base == 0:
            here = here | (at == cols + h)
        return here

    mine = sub * heads
    left_off = [[off_lanes(b, mine, 0, t) for t in range(2)] for b in range(2)]
    right_off = [[off_lanes(b, mine, HALF, t) for t in range(2)] for b in range(2)]
    kv_off = [
        [left_off[b][0], jnp.where(low, left_off[b][1], right_off[b][0]), right_off[b][1]]
        for b in range(2)
    ]

    for dst, src in ((sq, q_ref), (sk, k_ref), (sv, v_ref)):
        dst[0, :, :] = src[:, :LANES].astype(jnp.float32)
        dst[1, :, :HALF] = src[:, LANES:].astype(jnp.float32)

    row64 = lax.broadcasted_iota(jnp.int32, (strip, LANES), 0) * R2
    block0 = seq * rows
    wide_kv = [None] * 3
    wide_q = [None] * 2
    for a in range(subs):
        mid_kv = [None] * 3
        mid_q = [None] * 2
        for m in range(R1):
            j = a * R1 + m
            at = pl.ds(j, strip, stride=R2)
            to = pl.ds(m * phase + a * strip, strip)
            k0, k1 = sk[0, at, :], sk[1, at, :]
            v0, v1 = sv[0, at, :], sv[1, at, :]
            q0, q1 = sq[0, at, :], sq[1, at, :]
            v0 = pltpu.roll(v0, HALF, 1)
            v1 = pltpu.roll(v1, HALF, 1)
            q1 = jnp.where(low, q1, 1.0)
            t1 = jnp.where(low, k1, v0)
            t2 = jnp.where(low, v0, v1)
            dead = jnp.where(block0 + row64 + j < limit, 0.0, MASKED)
            qp[to, :LANES] = q0.astype(jnp.bfloat16)
            qp[to, LANES:] = q1.astype(jnp.bfloat16)
            kx[to, :LANES] = k0.astype(jnp.bfloat16)
            kx[to, LANES:] = jnp.where(low, k1, dead).astype(jnp.bfloat16)
            vx[to, :LANES] = jnp.where(low, 1.0, v0).astype(jnp.bfloat16)
            vx[to, LANES:] = t2.astype(jnp.bfloat16)
            for i, tile in enumerate((k0, t1, t2)):
                mid_kv[i] = tile if m == 0 else jnp.where(kv_off[0][i] == m, tile, mid_kv[i])
                wide_kv[i] = tile if j == 0 else jnp.where(kv_off[1][i] == j, tile, wide_kv[i])
            for i, tile in enumerate((q0, q1)):
                mid_q[i] = tile if m == 0 else jnp.where(left_off[0][i] == m, tile, mid_q[i])
                wide_q[i] = tile if j == 0 else jnp.where(left_off[1][i] == j, tile, wide_q[i])
        to = pl.ds((a % 2) * strip, strip)
        for i in range(3):
            mid[pos, a // 2, to, i * LANES:(i + 1) * LANES] = mid_kv[i].astype(jnp.bfloat16)
        for i in range(2):
            qm[pl.ds(a * strip, strip), i * LANES:(i + 1) * LANES] = mid_q[i].astype(jnp.bfloat16)
    for i in range(3):
        wide[seq, :, i * LANES:(i + 1) * LANES] = wide_kv[i].astype(jnp.bfloat16)
    for i in range(2):
        qw[:, i * LANES:(i + 1) * LANES] = wide_q[i].astype(jnp.bfloat16)

    pl.semaphore_wait(barrier, n_seq - 1 + len(bits))

    def wide_copy(origin, step):
        return pltpu.make_async_remote_copy(
            src_ref=wide.at[origin], dst_ref=wide.at[origin],
            send_sem=wide_send.at[step], recv_sem=wide_recv.at[step],
            device_id={"seq": lax.rem(seq + step, n_seq)}, device_id_type=MESH,
        )

    for step in range(1, n_seq):
        wide_copy(seq, step).start()

    def mid_copy(origin, chunk, rightward):
        way = 0 if rightward else 1
        target = seq + 1 if rightward else seq - 1
        return pltpu.make_async_remote_copy(
            src_ref=mid.at[origin, chunk], dst_ref=mid.at[origin, chunk],
            send_sem=mid_send.at[way, origin, chunk], recv_sem=mid_recv.at[origin, chunk],
            device_id={"seq": target}, device_id_type=MESH,
        )

    for chunk in range(2):
        @pl.when(has_right)
        def _():
            mid_copy(pos, chunk, True).start()

        @pl.when(has_left)
        def _():
            mid_copy(pos, chunk, False).start()

    def relay(dist, chunk):
        @pl.when(pos - dist >= 0)
        def _():
            mid_copy(pos - dist, chunk, True).wait_recv()

            @pl.when(has_right)
            def _():
                mid_copy(pos - dist, chunk, True).start()

        @pl.when(pos + dist < GROUP)
        def _():
            mid_copy(pos + dist, chunk, False).wait_recv()

            @pl.when(has_left)
            def _():
                mid_copy(pos + dist, chunk, False).start()

    for d in range(n_sub):
        wl[d, pl.ds(cols, HALF), :] = jnp.zeros((HALF, cols), jnp.bfloat16)
        wr[d, pl.ds(0, HALF), :] = jnp.zeros((HALF, cols), jnp.bfloat16)
    for s in range(n_sub):
        @pl.when(sub == s)
        def _():
            for d in range(n_sub):
                part = w_ref[d * cols:(d + 1) * cols, s * cols:(s + 1) * cols]
                wl[d, pl.ds(0, cols), :] = part
                wr[d, pl.ds(HALF, cols), :] = part

    contract_last = (((1,), (1,)), ((), ()))

    def attend(q_blk, keys, values, h, before=None):
        masked_q = jnp.where(head_mask(h, 0), q_blk.astype(jnp.float32), 0.0).astype(jnp.bfloat16)
        scores = lax.dot_general(masked_q, keys, contract_last, preferred_element_type=jnp.float32)
        peak = jnp.max(scores, axis=1, keepdims=True)
        if before is not None:
            peak = jnp.maximum(peak, before)
        probs = jnp.exp2((scores - peak) * EXP_SCALE).astype(jnp.bfloat16)
        return peak, jnp.dot(probs, values, preferred_element_type=jnp.float32)

    def near_step(m, carry):
        at = pl.ds(pl.multiple_of(m * phase, phase), phase)
        q_blk = qp[at, :]
        acc = top = mass = None
        for h in range(heads):
            peak, out = attend(q_blk, kx[...], vx[...], h)
            here = head_mask(h, HALF)
            total = out[:, 0:1]
            shape = out.shape
            if h == 0:
                acc, top, mass = out, jnp.broadcast_to(peak, shape), jnp.broadcast_to(total, shape)
            else:
                acc = jnp.where(here, out, acc)
                top = jnp.where(here, peak, top)
                mass = jnp.where(here, total, mass)
        st_a[at, :] = acc
        st_m[at, :] = top
        st_l[at, :] = mass

        @pl.when(m == 2)
        def _():
            relay(1, 0)

        return carry

    lax.fori_loop(0, R1, near_step, 0)
    relay(1, 1)

    def merge(q_blk, keys, values, top, mass, acc):
        for h in range(heads):
            here = head_mask(h, HALF)
            before = jnp.max(jnp.where(here, top, -3e38), axis=1, keepdims=True)
            peak, out = attend(q_blk, keys, values, h, before)
            fade = jnp.exp2((before - peak) * EXP_SCALE)
            total = out[:, 0:1]
            acc = jnp.where(here, acc * fade + out, acc)
            mass = jnp.where(here, mass * fade + total, mass)
            top = jnp.where(here, peak, top)
        return top, mass, acc

    r_off = [jnp.concatenate(right_off[b], axis=1) for b in range(2)]
    wide_lane_off = left_off[1][1]
    for step in range(1, n_seq):
        wide_copy(lax.rem(seq + n_seq - step, n_seq), step).wait_recv()
    for o in range(n_seq):
        at = pl.ds(o * strip, strip)
        tile1 = wide[o, :, LANES:2 * LANES].astype(jnp.float32)
        dead = jnp.where(o * rows + row64 + wide_lane_off < limit, 0.0, MASKED)
        wk[at, :LANES] = wide[o, :, :LANES]
        wk[at, LANES:] = jnp.where(low, tile1, dead).astype(jnp.bfloat16)
        wv[at, :LANES] = jnp.where(low, 1.0, tile1).astype(jnp.bfloat16)
        wv[at, LANES:] = wide[o, :, 2 * LANES:]

    def strip_at(j):
        return pl.ds((j % R1) * phase + (j // R1) * strip, strip)

    wide_masks = [r_off[1] == j for j in range(R2)]
    state = [pick(wide_masks, [ref[strip_at(j), :] for j in range(R2)]) for ref in (st_m, st_l, st_a)]
    state = merge(qw[...], wk[...], wv[...], *state)
    for ref, new in zip((st_m, st_l, st_a), state):
        for j in range(R2):
            ref[strip_at(j), :] = jnp.where(wide_masks[j], new, ref[strip_at(j), :])

    def pack(slab, value):
        top_half, bot = value[:half_rows], value[half_rows:]
        moved = pltpu.roll(top_half, LANES + HALF, 1)
        xg[sub, slab, :, :LANES] = moved[:, :LANES].astype(jnp.bfloat16)
        xg[sub, slab, :, LANES:2 * LANES] = jnp.where(
            low, moved[:, LANES:], bot[:, :LANES]
        ).astype(jnp.bfloat16)
        xg[sub, slab, :, 2 * LANES:] = bot[:, LANES:].astype(jnp.bfloat16)

    def x_copy(at_bit, held, slab):
        bit = bits[at_bit]
        block = sub ^ held
        return pltpu.make_async_remote_copy(
            src_ref=xg.at[block, slab], dst_ref=xg.at[block, slab],
            send_sem=x_send.at[at_bit, held, slab], recv_sem=x_recv.at[held ^ bit, slab],
            device_id={"sub": sub ^ bit}, device_id_type=MESH,
        )

    def x_plan():
        held, plan = [0], []
        for at_bit, bit in enumerate(bits):
            plan += [(at_bit, x) for x in held]
            held = held + [x ^ bit for x in held]
        return plan

    def x_start(slab):
        for at_bit, x in x_plan():
            if x == 0:
                x_copy(at_bit, x, slab).start()

    def x_recv_wait(block, slab):
        pltpu.make_async_remote_copy(
            src_ref=xg.at[sub ^ block, slab], dst_ref=xg.at[sub ^ block, slab],
            send_sem=x_send.at[0, 0, slab], recv_sem=x_recv.at[block, slab],
            device_id={"sub": sub ^ block}, device_id_type=MESH,
        ).wait_recv()

    def x_forward(slab):
        waited = set()
        for at_bit, x in x_plan():
            if x:
                if x not in waited:
                    waited.add(x)
                    x_recv_wait(x, slab)
                x_copy(at_bit, x, slab).start()
        return waited

    def x_finish(slab, waited):
        for x in range(1, n_sub):
            if x not in waited:
                x_recv_wait(x, slab)

    mid_masks = [r_off[0] == m for m in range(R1)]
    for slab in range(1, R1):
        parts = []
        for m in range(R1):
            at = pl.ds(m * phase, phase)
            parts.append(st_a[at, :] / st_l[at, :])
        pack(slab, pick([mid_masks[(m - slab) % R1] for m in range(R1)], parts))
        x_start(slab)

    for chunk in range(2):
        relay(2, chunk)
    for chunk in range(2):
        relay(3, chunk)

    mid_lane_off = left_off[0][1]
    pair_row = lax.broadcasted_iota(jnp.int32, (half_rows, LANES), 0)
    pair_row = (pair_row % strip) * R2 + (pair_row // strip) * R1
    for o in range(GROUP):
        for chunk in range(2):
            at = pl.ds(o * phase + chunk * half_rows, half_rows)
            tile1 = mid[o, chunk, :, LANES:2 * LANES].astype(jnp.float32)
            place = (group0 + o) * rows + pair_row + (chunk * 2 * R1 + mid_lane_off)
            dead = jnp.where(place < limit, 0.0, MASKED)
            mk[at, :LANES] = mid[o, chunk, :, :LANES]
            mk[at, LANES:] = jnp.where(low, tile1, dead).astype(jnp.bfloat16)
            mv[at, :LANES] = jnp.where(low, 1.0, tile1).astype(jnp.bfloat16)
            mv[at, LANES:] = mid[o, chunk, :, 2 * LANES:]
    state = [
        pick(mid_masks, [ref[pl.ds(m * phase, phase), :] for m in range(R1)])
        for ref in (st_m, st_l, st_a)
    ]
    state = merge(qm[...], mk[...], mv[...], *state)
    pack(0, state[2] / state[1])
    x_start(0)

    done = {}
    for slab in (1, 2, 3, 0):
        done[slab] = x_forward(slab)
    for slab in (1, 2, 3, 0):
        x_finish(slab, done[slab])

    outs = [[None, None] for _ in range(R1)]
    for d in range(n_sub):
        offs = [
            jnp.concatenate([off_lanes(0, d * heads, base, t) for t in range(2)], axis=1)
            for base in (0, HALF)
        ]
        for half in range(2):
            take = slice(half * LANES, half * LANES + 2 * LANES)
            slabs = [xg[d, i, :, take].astype(jnp.float32) for i in range(R1)]
            weights = (wl, wr)[half][d]
            for m in range(R1):
                masks = [offs[half] == (m - i) % R1 for i in range(R1)]
                term = jnp.dot(
                    pick(masks, slabs).astype(jnp.bfloat16), weights,
                    preferred_element_type=jnp.float32,
                )
                outs[m][half] = term if d == 0 else outs[m][half] + term
    for m in range(R1):
        for half in range(2):
            for s in range(2):
                a = half * 2 + s
                res = outs[m][half][s * strip:(s + 1) * strip]
                at = pl.ds(a * R1 + m, strip, stride=R2)
                so[0, at, :] = res[:, :LANES]
                so[1, at, :HALF] = res[:, LANES:]
    keep = block0 + lax.broadcasted_iota(jnp.int32, (rows, 1), 0) < limit
    o_ref[:, :LANES] = jnp.where(keep, so[0, :, :], 0.0).astype(jnp.bfloat16)
    o_ref[:, LANES:] = jnp.where(keep, so[1, :, :HALF], 0.0).astype(jnp.bfloat16)

    for step in range(1, n_seq):
        wide_copy(seq, step).wait_send()
    for chunk in range(2):
        for o in range(GROUP):
            @pl.when(has_right & (pos >= o))
            def _():
                mid_copy(o, chunk, True).wait_send()

            @pl.when(has_left & (pos <= o))
            def _():
                mid_copy(o, chunk, False).wait_send()
    for slab in range(R1):
        for at_bit, x in x_plan():
            x_copy(at_bit, x, slab).wait_send()


def local(n_seq, n_sub, q_heads, k_heads, v_heads, w_out, offsets, valid):
    rows, cols = q_heads.shape
    heads = cols // HS
    phase, strip = rows // R1, rows // R2
    bf, f32 = jnp.bfloat16, jnp.float32
    n_bits = n_sub.bit_length() - 1
    assert cols == LANES + HALF and n_sub == 1 << n_bits
    vmem = pl.BlockSpec(memory_space=pltpu.VMEM)
    smem = pl.BlockSpec(memory_space=pltpu.SMEM)
    wide_all = n_seq * strip
    return pl.pallas_call(
        functools.partial(kernel, n_seq, n_sub, heads),
        out_shape=jax.ShapeDtypeStruct((rows, cols), bf),
        in_specs=[vmem] * 4 + [smem] * 2,
        out_specs=vmem,
        scratch_shapes=[
            pltpu.VMEM((2, rows, LANES), f32),
            pltpu.VMEM((2, rows, LANES), f32),
            pltpu.VMEM((2, rows, LANES), f32),
            pltpu.VMEM((rows, 2 * LANES), bf),
            pltpu.VMEM((rows, 2 * LANES), bf),
            pltpu.VMEM((rows, 2 * LANES), bf),
            pltpu.VMEM((phase, 2 * LANES), bf),
            pltpu.VMEM((strip, 2 * LANES), bf),
            pltpu.VMEM((n_seq, strip, 3 * LANES), bf),
            pltpu.VMEM((GROUP, 2, phase // 2, 3 * LANES), bf),
            pltpu.VMEM((wide_all, 2 * LANES), bf),
            pltpu.VMEM((wide_all, 2 * LANES), bf),
            pltpu.VMEM((GROUP * phase, 2 * LANES), bf),
            pltpu.VMEM((GROUP * phase, 2 * LANES), bf),
            pltpu.VMEM((rows, 2 * LANES), f32),
            pltpu.VMEM((rows, 2 * LANES), f32),
            pltpu.VMEM((rows, 2 * LANES), f32),
            pltpu.VMEM((n_sub, R1, phase // 2, 3 * LANES), bf),
            pltpu.VMEM((n_sub, 2 * LANES, cols), bf),
            pltpu.VMEM((n_sub, 2 * LANES, cols), bf),
            pltpu.VMEM((2, rows, LANES), f32),
            pltpu.SemaphoreType.DMA((n_seq,)),
            pltpu.SemaphoreType.DMA((n_seq,)),
            pltpu.SemaphoreType.DMA((2, GROUP, 2)),
            pltpu.SemaphoreType.DMA((GROUP, 2)),
            pltpu.SemaphoreType.DMA((n_bits, n_sub, R1)),
            pltpu.SemaphoreType.DMA((n_sub, R1)),
        ],
        compiler_params=pltpu.CompilerParams(
            collective_id=0, has_side_effects=True, vmem_limit_bytes=56 * 1024 * 1024
        ),
    )(q_heads, k_heads, v_heads, w_out, offsets, valid)


def solution(mesh):
    spread = P(("slides", "seq"), "sub")
    return jax.shard_map(
        functools.partial(local, mesh.shape["seq"], mesh.shape["sub"]),
        mesh=mesh,
        in_specs=(spread, spread, spread, P(), P(), P("slides")),
        out_specs=spread,
        check_vma=False,
    )
```

time: 162 us -> 41.7 us (0.26)
  local copies, waits for them, and re-layouts: 59.1 us -> 5.98 us
  waiting for transfers between devices: 36.9 us -> 0 us
  Pallas kernels: 0 us -> 34.8 us
  other arithmetic: 23.1 us -> 0 us
  between operations: 14.3 us -> 0.74 us
  matrix products: 12 us -> 0 us
  blocking collectives: 11.8 us -> 0 us
  starting transfers between devices: 2.59 us -> 0 us
    pallas_call x0 -> x1, Pallas kernels: none -> 34.8 us  [local(): pl.pallas_call(functools.partial(kernel, n_seq, n_sub, heads), out_shape=...]
    all_gather x1 -> x0, waiting for transfers between devices: 20.2 us -> none  [local(): lax.all_gather(attn, 'sub', axis=1, tiled=True)]
    broadcast_in_dim x18 -> x0, local copies, waits for them, and re-layouts: 19.1 us -> none  [the longest x6 10.4 us: spread_back(): jnp.where(onehot[..., None], numer[:, None, :, :], 0.0)]
    reduce_sum x6 -> x0, other arithmetic: 17.1 us -> none  [the longest x2 11.1 us: pick_rows(): jnp.sum(jnp.where(onehot[None, :, :, None], grouped, jnp.zeros((), source...]
    dynamic_update_slice x6 -> x0, local copies, waits for them, and re-layouts: 17 us -> none  [block_stats(): lax.map(attend, q_sel.reshape(n_query // width, width, q_sel.shape[1], q_...]
    ppermute x2 -> x0, waiting for transfers between devices: 16.7 us -> none  [swapped(): return lax.ppermute(value, axis, pairs)]
    dot_general x9 -> x0, matrix products: 12 us -> none  [the longest x4 5.13 us: attend(): jnp.einsum('hqk,khd->qhd', probs.astype(jnp.bfloat16), v_sel, preferred_e...]
    all_gather x1 -> x0, blocking collectives: 11.8 us -> none  [local(): piece = lax.all_gather(kv_wide, 'seq', axis=0, tiled=True)]
  transfers between devices with their start and end apart: 3 -> 0, of which waited for: 2 -> 0; matrix products, arithmetic and copies ran while one was open for 32% -> 0% of each run, Pallas kernels for 0% -> 0%
where the time goes in v1:
time: 41.7 us; the launch traced here: 41.5 us
  Pallas kernels  34.8 us (83%)
  local copies, waits for them, and re-layouts  5.98 us (14%)
  between operations  0.74 us (2%)
    pallas_call x1, Pallas kernels, local(): pl.pallas_call(functools.partial(kernel, n_seq, n_sub, heads), out_shape=...  34.8 us
    unnamed x7, local copies, waits for them, and re-layouts  4 us
    pallas_call x1, local copies, waits for them, and re-layouts, local(): pl.pallas_call(functools.partial(kernel, n_seq, n_sub, heads), out_shape=...  1.98 us

profile of v1, /device:TPU:1, one launch (start us, length us, event | category | flops | bytes accessed | tf_op | source)
XLA Modules:
  0.0 41.5 jit_solution(10105069723601586751)
XLA Ops:
  0.0 0.0 copy-start.1
  0.0 0.0 copy-start
  0.7 2.0 %copy.7.q_ref = bf16[1024,192]{1,0:T(8,128)(2,1)} copy(bf16[1024,192]{0,1:T(8,128)(2,1)} %param.6) | data formatting | bytes 786432 | tf_op args[0]
  2.7 0.0 copy-done
  2.7 1.0 %copy.8.k_ref = bf16[1024,192]{1,0:T(8,128)(2,1)} copy(bf16[1024,192]{0,1:T(8,128)(2,1)S(1)} %copy-done) | data formatting | bytes 786432 | tf_op args[1]
  3.7 0.0 copy-done.1
  3.7 1.0 %copy.9.v_ref = bf16[1024,192]{1,0:T(8,128)(2,1)} copy(bf16[1024,192]{0,1:T(8,128)(2,1)S(1)} %copy-done.1) | data formatting | bytes 786432 | tf_op args[2]
  4.7 34.8 %shard_map.64 = bf16[1024,192]{1,0:T(8,128)(2,1)} custom-call(bf16[1024,192]{1,0:T(8,128)(2,1)} %copy.7.q_ref, bf16[1024,192]{1,0:T(8,128)(2,1)} %copy.8.k_ref, bf16[1024,192]{1,0:T(8,128)(2,1)} %copy.9.v_ref, bf16[768,768]{1,0:T(8,128)(2,1)} %w_ref.1, s32[2,16]{1,0:T(2,128)} %off_ref.1, s32[1]{0:T(128)S(6)} %copy.11.valid_ref), custom_call_target="tpu_custom_call" | custom-call | tf_op jit(solution)/shard_map/pallas_call | solution.py:410
  39.5 2.0 %copy.10 = bf16[1024,192]{0,1:T(8,128)(2,1)} copy(bf16[1024,192]{1,0:T(8,128)(2,1)} %shard_map.64) | data formatting | bytes 786432 | tf_op jit(solution)/shard_map/pallas_call | solution.py:410
Async XLA Ops:
  0.0 3.7 %copy-start.1 = (bf16[1024,192]{0,1:T(8,128)(2,1)S(1)}, bf16[1024,192]{0,1:T(8,128)(2,1)}, u32[]{:S(2)}) copy-start(bf16[1024,192]{0,1:T(8,128)(2,1)} %param.8) | copy-start | bytes 1179652
  0.0 2.7 %copy-start = (bf16[1024,192]{0,1:T(8,128)(2,1)S(1)}, bf16[1024,192]{0,1:T(8,128)(2,1)}, u32[]{:S(2)}) copy-start(bf16[1024,192]{0,1:T(8,128)(2,1)} %param.7) | copy-start | bytes 1179652

commit v2 on v1

--- a/solution.py
+++ b/solution.py
@@ -28,11 +28,11 @@
 def kernel(
     n_seq, n_sub, heads,
     q_ref, k_ref, v_ref, w_ref, off_ref, valid_ref, o_ref,
-    sq, sk, sv, qp, kx, vx, qm, qw, wide, mid, wk, wv, mk, mv,
+    qp, kx, vx, qm, qw, wide, mid, wk, wv, mk, mv,
     st_m, st_l, st_a, xg, wl, wr, so,
     wide_send, wide_recv, mid_send, mid_recv, x_send, x_recv,
 ):
-    rows = q_ref.shape[0]
+    rows = q_ref.shape[1]
     cols = heads * HS
     phase = rows // R1
     strip = rows // R2
@@ -81,53 +81,60 @@
         for b in range(2)
     ]
 
-    for dst, src in ((sq, q_ref), (sk, k_ref), (sv, v_ref)):
-        dst[0, :, :] = src[:, :LANES].astype(jnp.float32)
-        dst[1, :, :HALF] = src[:, LANES:].astype(jnp.float32)
+    square = R2 * R2
+    at_row = lax.broadcasted_iota(jnp.int32, (square, square), 0)
+    at_tok = lax.broadcasted_iota(jnp.int32, (square, square), 1)
+    one_hot = jnp.where(at_tok == at_row % R2 * R2 + at_row // R2, 1.0, 0.0).astype(jnp.bfloat16)
+    contract_last = (((1,), (1,)), ((), ()))
+    contract_first = (((0,), (0,)), ((), ()))
 
     row64 = lax.broadcasted_iota(jnp.int32, (strip, LANES), 0) * R2
+    row16 = lax.broadcasted_iota(jnp.int32, (R2, LANES), 0) * R2
     block0 = seq * rows
-    wide_kv = [None] * 3
-    wide_q = [None] * 2
-    for a in range(subs):
-        mid_kv = [None] * 3
-        mid_q = [None] * 2
-        for m in range(R1):
-            j = a * R1 + m
-            at = pl.ds(j, strip, stride=R2)
-            to = pl.ds(m * phase + a * strip, strip)
-            k0, k1 = sk[0, at, :], sk[1, at, :]
-            v0, v1 = sv[0, at, :], sv[1, at, :]
-            q0, q1 = sq[0, at, :], sq[1, at, :]
-            v0 = pltpu.roll(v0, HALF, 1)
-            v1 = pltpu.roll(v1, HALF, 1)
-            q1 = jnp.where(low, q1, 1.0)
-            t1 = jnp.where(low, k1, v0)
-            t2 = jnp.where(low, v0, v1)
-            dead = jnp.where(block0 + row64 + j < limit, 0.0, MASKED)
-            qp[to, :LANES] = q0.astype(jnp.bfloat16)
-            qp[to, LANES:] = q1.astype(jnp.bfloat16)
-            kx[to, :LANES] = k0.astype(jnp.bfloat16)
-            kx[to, LANES:] = jnp.where(low, k1, dead).astype(jnp.bfloat16)
-            vx[to, :LANES] = jnp.where(low, 1.0, v0).astype(jnp.bfloat16)
-            vx[to, LANES:] = t2.astype(jnp.bfloat16)
-            for i, tile in enumerate((k0, t1, t2)):
-                mid_kv[i] = tile if m == 0 else jnp.where(kv_off[0][i] == m, tile, mid_kv[i])
-                wide_kv[i] = tile if j == 0 else jnp.where(kv_off[1][i] == j, tile, wide_kv[i])
-            for i, tile in enumerate((q0, q1)):
-                mid_q[i] = tile if m == 0 else jnp.where(left_off[0][i] == m, tile, mid_q[i])
-                wide_q[i] = tile if j == 0 else jnp.where(left_off[1][i] == j, tile, wide_q[i])
-        to = pl.ds((a % 2) * strip, strip)
-        for i in range(3):
-            mid[pos, a // 2, to, i * LANES:(i + 1) * LANES] = mid_kv[i].astype(jnp.bfloat16)
-        for i in range(2):
-            qm[pl.ds(a * strip, strip), i * LANES:(i + 1) * LANES] = mid_q[i].astype(jnp.bfloat16)
-    for i in range(3):
-        wide[seq, :, i * LANES:(i + 1) * LANES] = wide_kv[i].astype(jnp.bfloat16)
-    for i in range(2):
-        qw[:, i * LANES:(i + 1) * LANES] = wide_q[i].astype(jnp.bfloat16)
-
-    pl.semaphore_wait(barrier, n_seq - 1 + len(bits))
+    with jax.named_scope("load"):
+        for blk in range(rows // square):
+            toks = pl.ds(blk * square, square)
+            kv_t = jnp.concatenate([k_ref[:, toks], v_ref[:, toks]], axis=0)
+            q_t = jnp.concatenate([q_ref[:, toks], jnp.ones((HALF, square), jnp.bfloat16)], axis=0)
+            kv = lax.dot_general(one_hot, kv_t, contract_last, preferred_element_type=jnp.float32)
+            qs = lax.dot_general(one_hot, q_t, contract_last, preferred_element_type=jnp.float32)
+            wide_kv = [None] * 3
+            wide_q = [None] * 2
+            for a in range(subs):
+                mid_kv = [None] * 3
+                mid_q = [None] * 2
+                for m in range(R1):
+                    j = a * R1 + m
+                    to = pl.ds(m * phase + a * strip + blk * R2, R2)
+                    kv_j, q_j = kv[j * R2:(j + 1) * R2], qs[j * R2:(j + 1) * R2]
+                    tiles = [kv_j[:, i * LANES:(i + 1) * LANES] for i in range(3)]
+                    q_tiles = [q_j[:, i * LANES:(i + 1) * LANES] for i in range(2)]
+                    dead = jnp.where(block0 + blk * square + row16 + j < limit, 0.0, MASKED)
+                    qp[to, :] = q_j.astype(jnp.bfloat16)
+                    kx[to, :LANES] = tiles[0].astype(jnp.bfloat16)
+                    kx[to, LANES:] = jnp.where(low, tiles[1], dead).astype(jnp.bfloat16)
+                    vx[to, :LANES] = jnp.where(low, 1.0, tiles[1]).astype(jnp.bfloat16)
+                    vx[to, LANES:] = tiles[2].astype(jnp.bfloat16)
+                    for i, tile in enumerate(tiles):
+                        mid_kv[i] = tile if m == 0 else jnp.where(kv_off[0][i] == m, tile, mid_kv[i])
+                        wide_kv[i] = tile if j == 0 else jnp.where(kv_off[1][i] == j, tile, wide_kv[i])
+                    for i, tile in enumerate(q_tiles):
+                        mid_q[i] = tile if m == 0 else jnp.where(left_off[0][i] == m, tile, mid_q[i])
+                        wide_q[i] = tile if j == 0 else jnp.where(left_off[1][i] == j, tile, wide_q[i])
+                to = pl.ds((a % 2) * strip + blk * R2, R2)
+                for i in range(3):
+                    mid[pos, a // 2, to, i * LANES:(i + 1) * LANES] = mid_kv[i].astype(jnp.bfloat16)
+                to = pl.ds(a * strip + blk * R2, R2)
+                for i in range(2):
+                    qm[to, i * LANES:(i + 1) * LANES] = mid_q[i].astype(jnp.bfloat16)
+            to = pl.ds(blk * R2, R2)
+            for i in range(3):
+                wide[seq, to, i * LANES:(i + 1) * LANES] = wide_kv[i].astype(jnp.bfloat16)
+            for i in range(2):
+                qw[to, i * LANES:(i + 1) * LANES] = wide_q[i].astype(jnp.bfloat16)
+
+    with jax.named_scope("barrier"):
+        pl.semaphore_wait(barrier, n_seq - 1 + len(bits))
 
     def wide_copy(origin, step):
         return pltpu.make_async_remote_copy(
@@ -174,18 +181,17 @@
             def _():
                 mid_copy(pos + dist, chunk, False).start()
 
-    for d in range(n_sub):
-        wl[d, pl.ds(cols, HALF), :] = jnp.zeros((HALF, cols), jnp.bfloat16)
-        wr[d, pl.ds(0, HALF), :] = jnp.zeros((HALF, cols), jnp.bfloat16)
-    for s in range(n_sub):
-        @pl.when(sub == s)
-        def _():
-            for d in range(n_sub):
-                part = w_ref[d * cols:(d + 1) * cols, s * cols:(s + 1) * cols]
-                wl[d, pl.ds(0, cols), :] = part
-                wr[d, pl.ds(HALF, cols), :] = part
-
-    contract_last = (((1,), (1,)), ((), ()))
+    with jax.named_scope("weights"):
+        for d in range(n_sub):
+            wl[d, pl.ds(cols, HALF), :] = jnp.zeros((HALF, cols), jnp.bfloat16)
+            wr[d, pl.ds(0, HALF), :] = jnp.zeros((HALF, cols), jnp.bfloat16)
+        for s in range(n_sub):
+            @pl.when(sub == s)
+            def _():
+                for d in range(n_sub):
+                    part = w_ref[d * cols:(d + 1) * cols, s * cols:(s + 1) * cols]
+                    wl[d, pl.ds(0, cols), :] = part
+                    wr[d, pl.ds(HALF, cols), :] = part
 
     def attend(q_blk, keys, values, h, before=None):
         masked_q = jnp.where(head_mask(h, 0), q_blk.astype(jnp.float32), 0.0).astype(jnp.bfloat16)
@@ -221,7 +227,8 @@
 
         return carry
 
-    lax.fori_loop(0, R1, near_step, 0)
+    with jax.named_scope("near"):
+        lax.fori_loop(0, R1, near_step, 0)
     relay(1, 1)
 
     def merge(q_blk, keys, values, top, mass, acc):
@@ -238,8 +245,9 @@
 
     r_off = [jnp.concatenate(right_off[b], axis=1) for b in range(2)]
     wide_lane_off = left_off[1][1]
-    for step in range(1, n_seq):
-        wide_copy(lax.rem(seq + n_seq - step, n_seq), step).wait_recv()
+    with jax.named_scope("wide_wait"):
+        for step in range(1, n_seq):
+            wide_copy(lax.rem(seq + n_seq - step, n_seq), step).wait_recv()
     for o in range(n_seq):
         at = pl.ds(o * strip, strip)
         tile1 = wide[o, :, LANES:2 * LANES].astype(jnp.float32)
@@ -252,12 +260,13 @@
     def strip_at(j):
         return pl.ds((j % R1) * phase + (j // R1) * strip, strip)
 
-    wide_masks = [r_off[1] == j for j in range(R2)]
-    state = [pick(wide_masks, [ref[strip_at(j), :] for j in range(R2)]) for ref in (st_m, st_l, st_a)]
-    state = merge(qw[...], wk[...], wv[...], *state)
-    for ref, new in zip((st_m, st_l, st_a), state):
-        for j in range(R2):
-            ref[strip_at(j), :] = jnp.where(wide_masks[j], new, ref[strip_at(j), :])
+    with jax.named_scope("wide_merge"):
+        wide_masks = [r_off[1] == j for j in range(R2)]
+        state = [pick(wide_masks, [ref[strip_at(j), :] for j in range(R2)]) for ref in (st_m, st_l, st_a)]
+        state = merge(qw[...], wk[...], wv[...], *state)
+        for ref, new in zip((st_m, st_l, st_a), state):
+            for j in range(R2):
+                ref[strip_at(j), :] = jnp.where(wide_masks[j], new, ref[strip_at(j), :])
 
     def pack(slab, value):
         top_half, bot = value[:half_rows], value[half_rows:]
@@ -312,89 +321,98 @@
                 x_recv_wait(x, slab)
 
     mid_masks = [r_off[0] == m for m in range(R1)]
-    for slab in range(1, R1):
-        parts = []
-        for m in range(R1):
-            at = pl.ds(m * phase, phase)
-            parts.append(st_a[at, :] / st_l[at, :])
-        pack(slab, pick([mid_masks[(m - slab) % R1] for m in range(R1)], parts))
-        x_start(slab)
-
-    for chunk in range(2):
-        relay(2, chunk)
-    for chunk in range(2):
-        relay(3, chunk)
+    with jax.named_scope("slabs"):
+        for slab in range(1, R1):
+            parts = []
+            for m in range(R1):
+                at = pl.ds(m * phase, phase)
+                parts.append(st_a[at, :] / st_l[at, :])
+            pack(slab, pick([mid_masks[(m - slab) % R1] for m in range(R1)], parts))
+            x_start(slab)
+
+    with jax.named_scope("relays"):
+        for chunk in range(2):
+            relay(2, chunk)
+        for chunk in range(2):
+            relay(3, chunk)
 
     mid_lane_off = left_off[0][1]
     pair_row = lax.broadcasted_iota(jnp.int32, (half_rows, LANES), 0)
     pair_row = (pair_row % strip) * R2 + (pair_row // strip) * R1
-    for o in range(GROUP):
+    with jax.named_scope("mid_merge"):
+        for o in range(GROUP):
+            for chunk in range(2):
+                at = pl.ds(o * phase + chunk * half_rows, half_rows)
+                tile1 = mid[o, chunk, :, LANES:2 * LANES].astype(jnp.float32)
+                place = (group0 + o) * rows + pair_row + (chunk * 2 * R1 + mid_lane_off)
+                dead = jnp.where(place < limit, 0.0, MASKED)
+                mk[at, :LANES] = mid[o, chunk, :, :LANES]
+                mk[at, LANES:] = jnp.where(low, tile1, dead).astype(jnp.bfloat16)
+                mv[at, :LANES] = jnp.where(low, 1.0, tile1).astype(jnp.bfloat16)
+                mv[at, LANES:] = mid[o, chunk, :, 2 * LANES:]
+        state = [
+            pick(mid_masks, [ref[pl.ds(m * phase, phase), :] for m in range(R1)])
+            for ref in (st_m, st_l, st_a)
+        ]
+        state = merge(qm[...], mk[...], mv[...], *state)
+        pack(0, state[2] / state[1])
+        x_start(0)
+
+    with jax.named_scope("x_wait"):
+        done = {}
+        for slab in (1, 2, 3, 0):
+            done[slab] = x_forward(slab)
+        for slab in (1, 2, 3, 0):
+            x_finish(slab, done[slab])
+
+    with jax.named_scope("project"):
+        outs = [[None, None] for _ in range(R1)]
+        for d in range(n_sub):
+            offs = [
+                jnp.concatenate([off_lanes(0, d * heads, base, t) for t in range(2)], axis=1)
+                for base in (0, HALF)
+            ]
+            for half in range(2):
+                take = slice(half * LANES, half * LANES + 2 * LANES)
+                slabs = [xg[d, i, :, take].astype(jnp.float32) for i in range(R1)]
+                weights = (wl, wr)[half][d]
+                for m in range(R1):
+                    masks = [offs[half] == (m - i) % R1 for i in range(R1)]
+                    term = jnp.dot(
+                        pick(masks, slabs).astype(jnp.bfloat16), weights,
+                        preferred_element_type=jnp.float32,
+                    )
+                    outs[m][half] = term if d == 0 else outs[m][half] + term
+        for m in range(R1):
+            for half in range(2):
+                so[pl.ds(m * phase + half * half_rows, half_rows), :] = outs[m][half].astype(jnp.bfloat16)
+        for blk in range(rows // square):
+            picked = jnp.concatenate(
+                [
+                    so[pl.ds((j % R1) * phase + (j // R1) * strip + blk * R2, R2), :]
+                    for j in range(R2)
+                ],
+                axis=0,
+            )
+            res = lax.dot_general(picked, one_hot, contract_first, preferred_element_type=jnp.float32)
+            place = block0 + blk * square + lax.broadcasted_iota(jnp.int32, (1, square), 1)
+            o_ref[:, pl.ds(blk * square, square)] = jnp.where(place < limit, res, 0.0).astype(jnp.bfloat16)
+
+    with jax.named_scope("drain"):
+        for step in range(1, n_seq):
+            wide_copy(seq, step).wait_send()
         for chunk in range(2):
-            at = pl.ds(o * phase + chunk * half_rows, half_rows)
-            tile1 = mid[o, chunk, :, LANES:2 * LANES].astype(jnp.float32)
-            place = (group0 + o) * rows + pair_row + (chunk * 2 * R1 + mid_lane_off)
-            dead = jnp.where(place < limit, 0.0, MASKED)
-            mk[at, :LANES] = mid[o, chunk, :, :LANES]
-            mk[at, LANES:] = jnp.where(low, tile1, dead).astype(jnp.bfloat16)
-            mv[at, :LANES] = jnp.where(low, 1.0, tile1).astype(jnp.bfloat16)
-            mv[at, LANES:] = mid[o, chunk, :, 2 * LANES:]
-    state = [
-        pick(mid_masks, [ref[pl.ds(m * phase, phase), :] for m in range(R1)])
-        for ref in (st_m, st_l, st_a)
-    ]
-    state = merge(qm[...], mk[...], mv[...], *state)
-    pack(0, state[2] / state[1])
-    x_start(0)
-
-    done = {}
-    for slab in (1, 2, 3, 0):
-        done[slab] = x_forward(slab)
-    for slab in (1, 2, 3, 0):
-        x_finish(slab, done[slab])
-
-    outs = [[None, None] for _ in range(R1)]
-    for d in range(n_sub):
-        offs = [
-            jnp.concatenate([off_lanes(0, d * heads, base, t) for t in range(2)], axis=1)
-            for base in (0, HALF)
-        ]
-        for half in range(2):
-            take = slice(half * LANES, half * LANES + 2 * LANES)
-            slabs = [xg[d, i, :, take].astype(jnp.float32) for i in range(R1)]
-            weights = (wl, wr)[half][d]
-            for m in range(R1):
-                masks = [offs[half] == (m - i) % R1 for i in range(R1)]
-                term = jnp.dot(
-                    pick(masks, slabs).astype(jnp.bfloat16), weights,
-                    preferred_element_type=jnp.float32,
-                )
-                outs[m][half] = term if d == 0 else outs[m][half] + term
-    for m in range(R1):
-        for half in range(2):
-            for s in range(2):
-                a = half * 2 + s
-                res = outs[m][half][s * strip:(s + 1) * strip]
-                at = pl.ds(a * R1 + m, strip, stride=R2)
-                so[0, at, :] = res[:, :LANES]
-                so[1, at, :HALF] = res[:, LANES:]
-    keep = block0 + lax.broadcasted_iota(jnp.int32, (rows, 1), 0) < limit
-    o_ref[:, :LANES] = jnp.where(keep, so[0, :, :], 0.0).astype(jnp.bfloat16)
-    o_ref[:, LANES:] = jnp.where(keep, so[1, :, :HALF], 0.0).astype(jnp.bfloat16)
-
-    for step in range(1, n_seq):
-        wide_copy(seq, step).wait_send()
-    for chunk in range(2):
-        for o in range(GROUP):
-            @pl.when(has_right & (pos >= o))
-            def _():
-                mid_copy(o, chunk, True).wait_send()
-
-            @pl.when(has_left & (pos <= o))
-            def _():
-                mid_copy(o, chunk, False).wait_send()
-    for slab in range(R1):
-        for at_bit, x in x_plan():
-            x_copy(at_bit, x, slab).wait_send()
+            for o in range(GROUP):
+                @pl.when(has_right & (pos >= o))
+                def _():
+                    mid_copy(o, chunk, True).wait_send()
+
+                @pl.when(has_left & (pos <= o))
+                def _():
+                    mid_copy(o, chunk, False).wait_send()
+        for slab in range(R1):
+            for at_bit, x in x_plan():
+                x_copy(at_bit, x, slab).wait_send()
 
 
 def local(n_seq, n_sub, q_heads, k_heads, v_heads, w_out, offsets, valid):
@@ -409,13 +427,10 @@
     wide_all = n_seq * strip
     return pl.pallas_call(
         functools.partial(kernel, n_seq, n_sub, heads),
-        out_shape=jax.ShapeDtypeStruct((rows, cols), bf),
+        out_shape=jax.ShapeDtypeStruct((cols, rows), bf),
         in_specs=[vmem] * 4 + [smem] * 2,
         out_specs=vmem,
         scratch_shapes=[
-            pltpu.VMEM((2, rows, LANES), f32),
-            pltpu.VMEM((2, rows, LANES), f32),
-            pltpu.VMEM((2, rows, LANES), f32),
             pltpu.VMEM((rows, 2 * LANES), bf),
             pltpu.VMEM((rows, 2 * LANES), bf),
             pltpu.VMEM((rows, 2 * LANES), bf),
@@ -433,7 +448,7 @@
             pltpu.VMEM((n_sub, R1, phase // 2, 3 * LANES), bf),
             pltpu.VMEM((n_sub, 2 * LANES, cols), bf),
             pltpu.VMEM((n_sub, 2 * LANES, cols), bf),
-            pltpu.VMEM((2, rows, LANES), f32),
+            pltpu.VMEM((rows, cols), bf),
             pltpu.SemaphoreType.DMA((n_seq,)),
             pltpu.SemaphoreType.DMA((n_seq,)),
             pltpu.SemaphoreType.DMA((2, GROUP, 2)),
@@ -444,7 +459,7 @@
         compiler_params=pltpu.CompilerParams(
             collective_id=0, has_side_effects=True, vmem_limit_bytes=56 * 1024 * 1024
         ),
-    )(q_heads, k_heads, v_heads, w_out, offsets, valid)
+    )(q_heads.T, k_heads.T, v_heads.T, w_out, offsets, valid).T
 
 
 def solution(mesh):

time: 41.7 us -> 37 us (0.89)
  local copies, waits for them, and re-layouts: 5.98 us -> 1.77 us
    unnamed x7 -> x1, local copies, waits for them, and re-layouts: 4 us -> 1.77 us
    pallas_call x1 -> x0, local copies, waits for them, and re-layouts: 1.98 us -> none  [local(): pl.pallas_call(functools.partial(kernel, n_seq, n_sub, heads), out_shape=...]
where the time goes in v2:
time: 37 us; the launch traced here: 36.8 us
  Pallas kernels  34.4 us (93%)
  local copies, waits for them, and re-layouts  1.77 us (5%)
  between operations  0.66 us (2%)
    pallas_call x1, Pallas kernels, local(): pl.pallas_call(functools.partial(kernel, n_seq, n_sub, heads), out_shape=...  34.4 us
    unnamed x1, local copies, waits for them, and re-layouts  1.77 us

profile of v2, /device:TPU:1, one launch (start us, length us, event | category | flops | bytes accessed | tf_op | source)
XLA Modules:
  0.0 36.8 jit_solution(16462005180940534317)
XLA Ops:
  0.7 34.4 %shard_map.64 = bf16[192,1024]{1,0:T(8,128)(2,1)} custom-call(bf16[192,1024]{1,0:T(8,128)(2,1)} %bitcast.5, bf16[192,1024]{1,0:T(8,128)(2,1)} %bitcast.6, bf16[192,1024]{1,0:T(8,128)(2,1)} %bitcast.7, bf16[768,768]{1,0:T(8,128)(2,1)} %w_ref.1, s32[2,16]{1,0:T(2,128)} %off_ref.1, s32[1]{0:T(128)S(6)} %copy.8.valid_ref), custom_call_target="tpu_custom_call" | custom-call | tf_op jit(solution)/shard_map/pallas_call | solution.py:428
  35.0 1.8 %copy.9 = bf16[1024,192]{0,1:T(8,128)(2,1)} copy(bf16[1024,192]{0,1:T(8,128)(2,1)} %bitcast.4) | data formatting | bytes 786432

commit v3 on v2

v3 whole, which is shorter than its diff:
```python
import functools

import jax
import jax.numpy as jnp
from jax import lax
from jax.experimental import pallas as pl
from jax.experimental.pallas import tpu as pltpu
from jax.sharding import PartitionSpec as P

HS = 48
GROUP = 4
R1 = 4
R2 = 16
LANES = 128
HALF = 64
MASKED = -1e30
MESH = pl.DeviceIdType.MESH
EXP_SCALE = HS ** (-0.5) * 1.4426950408889634


def pick(masks, parts):
    out = parts[-1]
    for mask, part in zip(masks[:-1], parts[:-1]):
        out = jnp.where(mask, part, out)
    return out


def kernel(
    n_seq, n_sub, heads,
    q_hbm, k_hbm, v_hbm, w_hbm, off_ref, valid_ref, o_ref,
    q_ref, k_ref, v_ref, w_ref,
    qp, kx, vx, qw, wide, mid, wk, wv, mk, mv,
    st_m, st_l, st_a, xg, xw, wl, wr, so, at_x,
    wide_send, wide_recv, mid_send, mid_recv, x_send, x_recv, in_sem,
):
    rows = q_ref.shape[1]
    cols = heads * HS
    phase = rows // R1
    strip = rows // R2
    subs = R2 // R1
    half_rows = phase // 2
    seq = lax.axis_index("seq")
    sub = lax.axis_index("sub")
    pos = lax.rem(seq, GROUP)
    group0 = seq - pos
    limit = valid_ref[0]
    has_left = pos > 0
    has_right = pos < GROUP - 1
    bits = [1 << b for b in reversed(range(n_sub.bit_length() - 1))]

    fetches = [
        pltpu.make_async_copy(src, dst, in_sem.at[i])
        for i, (src, dst) in enumerate(
            ((k_hbm, k_ref), (v_hbm, v_ref), (q_hbm, q_ref), (w_hbm, w_ref))
        )
    ]
    for fetch in fetches:
        fetch.start()
    barrier = pltpu.get_barrier_semaphore()
    for step in (1, n_seq - 1):
        pl.semaphore_signal(
            barrier, inc=1, device_id={"seq": lax.rem(seq + step, n_seq)}, device_id_type=MESH
        )
    for bit in bits:
        pl.semaphore_signal(barrier, inc=1, device_id={"sub": sub ^ bit}, device_id_type=MESH)

    lane = lax.broadcasted_iota(jnp.int32, (1, LANES), 1)
    low = lane < HALF

    def off_lanes(which, first_head, base, tile):
        at = lane + tile * LANES - base
        out = jnp.zeros((1, LANES), jnp.int32)
        for h in range(heads):
            here = ((at >= h * HS) & (at < (h + 1) * HS)) | (at == cols + h)
            out = jnp.where(here, off_ref[which, first_head + h], out)
        return out

    def head_mask(h, base, tiles=2):
        at = lax.broadcasted_iota(jnp.int32, (1, tiles * LANES), 1) - base
        here = (at >= h * HS) & (at < (h + 1) * HS)
        if base == 0:
            here = here | (at == cols + h)
        return here

    mine = sub * heads
    left_off = [[off_lanes(b, mine, 0, t) for t in range(2)] for b in range(2)]
    right_off = [[off_lanes(b, mine, HALF, t) for t in range(2)] for b in range(2)]
    kv_off = [
        [left_off[b][0], jnp.where(low, left_off[b][1], right_off[b][0]), right_off[b][1]]
        for b in range(2)
    ]

    square = R2 * R2
    at_row = lax.broadcasted_iota(jnp.int32, (square, square), 0)
    at_tok = lax.broadcasted_iota(jnp.int32, (square, square), 1)
    one_hot = jnp.where(at_tok == at_row % R2 * R2 + at_row // R2, 1.0, 0.0).astype(jnp.bfloat16)
    contract_last = (((1,), (1,)), ((), ()))
    contract_first = (((0,), (0,)), ((), ()))

    turned = [[lax.rem(off + s, R1) for off in left_off[0]] for s in range(R1)]
    row64 = lax.broadcasted_iota(jnp.int32, (strip, LANES), 0) * R2
    row16 = lax.broadcasted_iota(jnp.int32, (R2, LANES), 0) * R2
    block0 = seq * rows
    with jax.named_scope("load"):
        for fetch in fetches[:3]:
            fetch.wait()
        for blk in range(rows // square):
            toks = pl.ds(blk * square, square)
            kv_t = jnp.concatenate([k_ref[:, toks], v_ref[:, toks]], axis=0)
            q_t = jnp.concatenate([q_ref[:, toks], jnp.ones((HALF, square), jnp.bfloat16)], axis=0)
            kv = lax.dot_general(one_hot, kv_t, contract_last, preferred_element_type=jnp.float32)
            qs = lax.dot_general(one_hot, q_t, contract_last, preferred_element_type=jnp.float32)
            wide_kv = [None] * 3
            wide_q = [None] * 2
            for a in range(subs):
                mid_kv = [None] * 3
                slab_q = [[None] * 2 for _ in range(R1)]
                for m in range(R1):
                    j = a * R1 + m
                    to = pl.ds(m * phase + a * strip + blk * R2, R2)
                    kv_j, q_j = kv[j * R2:(j + 1) * R2], qs[j * R2:(j + 1) * R2]
                    tiles = [kv_j[:, i * LANES:(i + 1) * LANES] for i in range(3)]
                    q_tiles = [q_j[:, i * LANES:(i + 1) * LANES] for i in range(2)]
                    dead = jnp.where(block0 + blk * square + row16 + j < limit, 0.0, MASKED)
                    kx[to, :LANES] = tiles[0].astype(jnp.bfloat16)
                    kx[to, LANES:] = jnp.where(low, tiles[1], dead).astype(jnp.bfloat16)
                    vx[to, :LANES] = jnp.where(low, 1.0, tiles[1]).astype(jnp.bfloat16)
                    vx[to, LANES:] = tiles[2].astype(jnp.bfloat16)
                    for i, tile in enumerate(tiles):
                        mid_kv[i] = tile if m == 0 else jnp.where(kv_off[0][i] == m, tile, mid_kv[i])
                        wide_kv[i] = tile if j == 0 else jnp.where(kv_off[1][i] == j, tile, wide_kv[i])
                    for i, tile in enumerate(q_tiles):
                        for s in range(R1):
                            here = turned[s][i] == m
                            slab_q[s][i] = tile if m == 0 else jnp.where(here, tile, slab_q[s][i])
                        wide_q[i] = tile if j == 0 else jnp.where(left_off[1][i] == j, tile, wide_q[i])
                to = pl.ds((a % 2) * strip + blk * R2, R2)
                for i in range(3):
                    mid[pos, a // 2, to, i * LANES:(i + 1) * LANES] = mid_kv[i].astype(jnp.bfloat16)
                for s in range(R1):
                    to = pl.ds(s * phase + a * strip + blk * R2, R2)
                    for i in range(2):
                        qp[to, i * LANES:(i + 1) * LANES] = slab_q[s][i].astype(jnp.bfloat16)
            to = pl.ds(blk * R2, R2)
            for i in range(3):
                wide[seq, to, i * LANES:(i + 1) * LANES] = wide_kv[i].astype(jnp.bfloat16)
            for i in range(2):
                qw[to, i * LANES:(i + 1) * LANES] = wide_q[i].astype(jnp.bfloat16)

    with jax.named_scope("barrier"):
        pl.semaphore_wait(barrier, 2 + len(bits))

    def wide_copy(origin, rightward):
        target = seq + 1 if rightward else seq - 1
        return pltpu.make_async_remote_copy(
            src_ref=wide.at[origin], dst_ref=wide.at[origin],
            send_sem=wide_send.at[0 if rightward else 1, origin], recv_sem=wide_recv.at[origin],
            device_id={"seq": target}, device_id_type=MESH,
        )

    @pl.when(seq < n_seq - 1)
    def _():
        wide_copy(seq, True).start()

    @pl.when(seq > 0)
    def _():
        wide_copy(seq, False).start()

    def wide_relay(dist):
        @pl.when(seq - dist >= 0)
        def _():
            wide_copy(seq - dist, True).wait_recv()

            @pl.when(seq < n_seq - 1)
            def _():
                wide_copy(seq - dist, True).start()

        @pl.when(seq + dist < n_seq)
        def _():
            wide_copy(seq + dist, False).wait_recv()

            @pl.when(seq > 0)
            def _():
                wide_copy(seq + dist, False).start()

    def mid_copy(origin, chunk, rightward):
        way = 0 if rightward else 1
        target = seq + 1 if rightward else seq - 1
        return pltpu.make_async_remote_copy(
            src_ref=mid.at[origin, chunk], dst_ref=mid.at[origin, chunk],
            send_sem=mid_send.at[way, origin, chunk], recv_sem=mid_recv.at[origin, chunk],
            device_id={"seq": target}, device_id_type=MESH,
        )

    for chunk in range(2):
        @pl.when(has_right)
        def _():
            mid_copy(pos, chunk, True).start()

        @pl.when(has_left)
        def _():
            mid_copy(pos, chunk, False).start()

    def relay(dist, chunk):
        @pl.when(pos - dist >= 0)
        def _():
            mid_copy(pos - dist, chunk, True).wait_recv()

            @pl.when(has_right)
            def _():
                mid_copy(pos - dist, chunk, True).start()

        @pl.when(pos + dist < GROUP)
        def _():
            mid_copy(pos + dist, chunk, False).wait_recv()

            @pl.when(has_left)
            def _():
                mid_copy(pos + dist, chunk, False).start()

    with jax.named_scope("weights"):
        fetches[3].wait()
        for d in range(n_sub):
            wl[pl.ds(d * 2 * LANES + cols, HALF), :] = jnp.zeros((HALF, cols), jnp.bfloat16)
            wr[pl.ds(d * 2 * LANES, HALF), :] = jnp.zeros((HALF, cols), jnp.bfloat16)
        for s in range(n_sub):
            @pl.when(sub == s)
            def _():
                for d in range(n_sub):
                    part = w_ref[d * cols:(d + 1) * cols, s * cols:(s + 1) * cols]
                    wl[pl.ds(d * 2 * LANES, cols), :] = part
                    wr[pl.ds(d * 2 * LANES + HALF, cols), :] = part

    def attend(q_blk, keys, values, h, before=None):
        masked_q = jnp.where(head_mask(h, 0), q_blk.astype(jnp.float32), 0.0).astype(jnp.bfloat16)
        scores = lax.dot_general(masked_q, keys, contract_last, preferred_element_type=jnp.float32)
        peak = jnp.max(scores, axis=1, keepdims=True)
        if before is not None:
            peak = jnp.maximum(peak, before)
        probs = jnp.exp2((scores - peak) * EXP_SCALE).astype(jnp.bfloat16)
        return peak, jnp.dot(probs, values, preferred_element_type=jnp.float32)

    def pack(slab, value):
        dst = xw.at[sub] if slab is None else xg.at[sub, slab]
        top_half, bot = value[:value.shape[0] // 2], value[value.shape[0] // 2:]
        moved = pltpu.roll(top_half, LANES + HALF, 1)
        dst[:, :LANES] = moved[:, :LANES].astype(jnp.bfloat16)
        dst[:, LANES:2 * LANES] = jnp.where(
            low, moved[:, LANES:], bot[:, :LANES]
        ).astype(jnp.bfloat16)
        dst[:, 2 * LANES:] = bot[:, LANES:].astype(jnp.bfloat16)

    def x_ref(block, slab):
        return xw.at[block] if isinstance(slab, int) and slab == R1 else xg.at[block, slab]

    def x_copy(at_bit, held, slab):
        bit = bits[at_bit]
        ref = x_ref(sub ^ held, slab)
        return pltpu.make_async_remote_copy(
            src_ref=ref, dst_ref=ref,
            send_sem=x_send.at[at_bit, held, slab], recv_sem=x_recv.at[held ^ bit, slab],
            device_id={"sub": sub ^ bit}, device_id_type=MESH,
        )

    def x_plan():
        held, plan = [0], []
        for at_bit, bit in enumerate(bits):
            plan += [(at_bit, x) for x in held]
            held = held + [x ^ bit for x in held]
        return plan

    def x_start(slab):
        for at_bit, x in x_plan():
            if x == 0:
                x_copy(at_bit, x, slab).start()

    def x_recv_wait(block, slab):
        ref = x_ref(sub ^ block, slab)
        pltpu.make_async_remote_copy(
            src_ref=ref, dst_ref=ref,
            send_sem=x_send.at[0, 0, slab], recv_sem=x_recv.at[block, slab],
            device_id={"sub": sub ^ block}, device_id_type=MESH,
        ).wait_recv()

    def x_forward(slab):
        waited = set()
        for at_bit, x in x_plan():
            if x:
                if x not in waited:
                    waited.add(x)
                    x_recv_wait(x, slab)
                x_copy(at_bit, x, slab).start()
        return waited

    def x_finish(slab, waited):
        for x in range(1, n_sub):
            if x not in waited:
                x_recv_wait(x, slab)

    def near_step(it, carry):
        slab = lax.rem(it + 1, R1)
        at = pl.ds(pl.multiple_of(slab * phase, phase), phase)
        q_blk = qp[at, :]
        acc = top = mass = None
        for h in range(heads):
            peak, out = attend(q_blk, kx[...], vx[...], h)
            here = head_mask(h, HALF)
            total = out[:, 0:1]
            shape = out.shape
            if h == 0:
                acc, top, mass = out, jnp.broadcast_to(peak, shape), jnp.broadcast_to(total, shape)
            else:
                acc = jnp.where(here, out, acc)
                top = jnp.where(here, peak, top)
                mass = jnp.where(here, total, mass)
        st_a[at, :] = acc
        st_m[at, :] = top
        st_l[at, :] = mass

        @pl.when(it < R1 - 1)
        def _():
            pack(slab, acc / mass)
            x_start(slab)

        @pl.when(it == 1)
        def _():
            wide_relay(1)
            relay(1, 0)

        @pl.when(it == 2)
        def _():
            wide_relay(2)
            relay(1, 1)
            x_forward(1)

        @pl.when(it == 3)
        def _():
            for dist in range(3, n_seq):
                wide_relay(dist)
            relay(2, 0)
            x_forward(2)

        return carry

    with jax.named_scope("near"):
        lax.fori_loop(0, R1, near_step, 0)

    def merge(q_blk, keys, values, top, mass, acc):
        for h in range(heads):
            here = head_mask(h, HALF)
            before = jnp.max(jnp.where(here, top, -3e38), axis=1, keepdims=True)
            peak, out = attend(q_blk, keys, values, h, before)
            fade = jnp.exp2((before - peak) * EXP_SCALE)
            total = out[:, 0:1]
            acc = jnp.where(here, acc * fade + out, acc)
            mass = jnp.where(here, mass * fade + total, mass)
            top = jnp.where(here, peak, top)
        return top, mass, acc

    mid_lane_off = left_off[0][1]
    pair_row = lax.broadcasted_iota(jnp.int32, (half_rows, LANES), 0)
    pair_row = (pair_row % strip) * R2 + (pair_row // strip) * R1
    pair = GROUP // 2
    own_pair = lax.div(pos, pair)

    def mid_merge(which):
        for o in range(pair):
            origin = which * pair + o
            for chunk in range(2):
                to = pl.ds(o * phase + chunk * half_rows, half_rows)
                tile1 = mid[origin, chunk, :, LANES:2 * LANES].astype(jnp.float32)
                place = (group0 + origin) * rows + pair_row + (chunk * 2 * R1 + mid_lane_off)
                dead = jnp.where(place < limit, 0.0, MASKED)
                mk[to, :LANES] = mid[origin, chunk, :, :LANES]
                mk[to, LANES:] = jnp.where(low, tile1, dead).astype(jnp.bfloat16)
                mv[to, :LANES] = jnp.where(low, 1.0, tile1).astype(jnp.bfloat16)
                mv[to, LANES:] = mid[origin, chunk, :, 2 * LANES:]
        at = pl.ds(0, phase)
        return merge(qp[at, :], mk[...], mv[...], st_m[at, :], st_l[at, :], st_a[at, :])

    with jax.named_scope("mid_merge_own"):
        for ref, new in zip((st_m, st_l, st_a), mid_merge(own_pair)):
            ref[pl.ds(0, phase), :] = new
        relay(2, 1)
        x_forward(3)

    r_off = [jnp.concatenate(right_off[b], axis=1) for b in range(2)]
    wide_lane_off = left_off[1][1]
    for o in range(n_seq):
        at = pl.ds(o * strip, strip)
        tile1 = wide[o, :, LANES:2 * LANES].astype(jnp.float32)
        dead = jnp.where(o * rows + row64 + wide_lane_off < limit, 0.0, MASKED)
        wk[at, :LANES] = wide[o, :, :LANES]
        wk[at, LANES:] = jnp.where(low, tile1, dead).astype(jnp.bfloat16)
        wv[at, :LANES] = jnp.where(low, 1.0, tile1).astype(jnp.bfloat16)
        wv[at, LANES:] = wide[o, :, 2 * LANES:]

    with jax.named_scope("wide_merge"):
        slab_of = lax.rem(r_off[1] + R1 - r_off[0], R1)
        part_of = lax.div(r_off[1], R1)
        strip_of = slab_of * subs + part_of
        wide_masks = [strip_of == j for j in range(R2)]
        state = [
            pick(wide_masks, [ref[pl.ds(j * strip, strip), :] for j in range(R2)])
            for ref in (st_m, st_l, st_a)
        ]
        state = merge(qw[...], wk[...], wv[...], *state)
        for ref, new in zip((st_m, st_l, st_a), state):
            for j in range(subs):
                at = pl.ds(j * strip, strip)
                ref[at, :] = jnp.where(wide_masks[j], new, ref[at, :])
        wide_out = state[2] / state[1]
    with jax.named_scope("relays"):
        for chunk in range(2):
            relay(3, chunk)

    with jax.named_scope("mid_merge"):
        state = mid_merge(1 - own_pair)
        mid_out = state[2] / state[1]
        pack(0, mid_out)
        x_start(0)
        parts = [mid_out[a * strip:(a + 1) * strip] for a in range(subs)]
        shared = pick([part_of == a for a in range(subs)], parts)
        pack(None, jnp.where(slab_of == 0, shared, wide_out))
        x_start(R1)
    with jax.named_scope("x_wait"):
        relayed = {x for at_bit, x in x_plan() if x}
        done = {slab: relayed for slab in range(1, R1)}
        for slab in (0, R1):
            done[slab] = x_forward(slab)
        for slab in (1, 2, 3, 0, R1):
            x_finish(slab, done[slab])

    with jax.named_scope("project"):
        for d in range(n_sub):
            offs, wide_offs = [
                [
                    jnp.concatenate([off_lanes(b, d * heads, base, t) for t in range(2)], axis=1)
                    for base in (0, HALF)
                ]
                for b in range(2)
            ]
            first = xw[d, :, :2 * LANES].astype(jnp.float32)
            second = xw[d, :, LANES:].astype(jnp.float32)
            wide_rows = [
                jnp.concatenate([first, pltpu.roll(second, LANES + HALF, 1)], axis=0),
                jnp.concatenate([pltpu.roll(first, HALF, 1), second], axis=0),
            ]
            for half in range(2):
                take = slice(half * LANES, half * LANES + 2 * LANES)
                slabs = [xg[d, i, :, take].astype(jnp.float32) for i in range(R1)]
                spare = wide_rows[half]
                for m in range(R1):
                    masks = [offs[half] == (m - i) % R1 for i in range(R1)]
                    rows_m = pick(masks, slabs)
                    rows_m = jnp.concatenate(
                        [
                            jnp.where(
                                wide_offs[half] == (half * 2 + i) * R1 + m, spare,
                                rows_m[i * strip:(i + 1) * strip],
                            )
                            for i in range(2)
                        ],
                        axis=0,
                    )
                    at_x[half, pl.ds(m * half_rows, half_rows), pl.ds(d * 2 * LANES, 2 * LANES)] = (
                        rows_m.astype(jnp.bfloat16)
                    )
        for half in range(2):
            out = jnp.dot(at_x[half], (wl, wr)[half][...], preferred_element_type=jnp.float32)
            out = out.astype(jnp.bfloat16)
            for m in range(R1):
                to = pl.ds(m * phase + half * half_rows, half_rows)
                so[to, :] = out[m * half_rows:(m + 1) * half_rows]
        for blk in range(rows // square):
            picked = jnp.concatenate(
                [
                    so[pl.ds((j % R1) * phase + (j // R1) * strip + blk * R2, R2), :]
                    for j in range(R2)
                ],
                axis=0,
            )
            res = lax.dot_general(picked, one_hot, contract_first, preferred_element_type=jnp.float32)
            place = block0 + blk * square + lax.broadcasted_iota(jnp.int32, (1, square), 1)
            o_ref[:, pl.ds(blk * square, square)] = jnp.where(place < limit, res, 0.0).astype(jnp.bfloat16)

    with jax.named_scope("drain"):
        for o in range(n_seq):
            @pl.when((seq < n_seq - 1) & (seq >= o))
            def _():
                wide_copy(o, True).wait_send()

            @pl.when((seq > 0) & (seq <= o))
            def _():
                wide_copy(o, False).wait_send()
        for chunk in range(2):
            for o in range(GROUP):
                @pl.when(has_right & (pos >= o))
                def _():
                    mid_copy(o, chunk, True).wait_send()

                @pl.when(has_left & (pos <= o))
                def _():
                    mid_copy(o, chunk, False).wait_send()
        for slab in range(R1 + 1):
            for at_bit, x in x_plan():
                x_copy(at_bit, x, slab).wait_send()


def local(n_seq, n_sub, q_heads, k_heads, v_heads, w_out, offsets, valid):
    rows, cols = q_heads.shape
    heads = cols // HS
    phase, strip = rows // R1, rows // R2
    bf, f32 = jnp.bfloat16, jnp.float32
    n_bits = n_sub.bit_length() - 1
    assert cols == LANES + HALF and n_sub == 1 << n_bits
    vmem = pl.BlockSpec(memory_space=pltpu.VMEM)
    smem = pl.BlockSpec(memory_space=pltpu.SMEM)
    wide_all = n_seq * strip
    return pl.pallas_call(
        functools.partial(kernel, n_seq, n_sub, heads),
        out_shape=jax.ShapeDtypeStruct((cols, rows), bf),
        in_specs=[pl.BlockSpec(memory_space=pl.ANY)] * 4 + [smem] * 2,
        out_specs=vmem,
        scratch_shapes=[
            pltpu.VMEM((cols, rows), bf),
            pltpu.VMEM((cols, rows), bf),
            pltpu.VMEM((cols, rows), bf),
            pltpu.VMEM(w_out.shape, bf),
            pltpu.VMEM((rows, 2 * LANES), bf),
            pltpu.VMEM((rows, 2 * LANES), bf),
            pltpu.VMEM((rows, 2 * LANES), bf),
            pltpu.VMEM((strip, 2 * LANES), bf),
            pltpu.VMEM((n_seq, strip, 3 * LANES), bf),
            pltpu.VMEM((GROUP, 2, phase // 2, 3 * LANES), bf),
            pltpu.VMEM((wide_all, 2 * LANES), bf),
            pltpu.VMEM((wide_all, 2 * LANES), bf),
            pltpu.VMEM((GROUP // 2 * phase, 2 * LANES), bf),
            pltpu.VMEM((GROUP // 2 * phase, 2 * LANES), bf),
            pltpu.VMEM((rows, 2 * LANES), f32),
            pltpu.VMEM((rows, 2 * LANES), f32),
            pltpu.VMEM((rows, 2 * LANES), f32),
            pltpu.VMEM((n_sub, R1, phase // 2, 3 * LANES), bf),
            pltpu.VMEM((n_sub, strip // 2, 3 * LANES), bf),
            pltpu.VMEM((n_sub * 2 * LANES, cols), bf),
            pltpu.VMEM((n_sub * 2 * LANES, cols), bf),
            pltpu.VMEM((rows, cols), bf),
            pltpu.VMEM((2, rows // 2, n_sub * 2 * LANES), bf),
            pltpu.SemaphoreType.DMA((2, n_seq)),
            pltpu.SemaphoreType.DMA((n_seq,)),
            pltpu.SemaphoreType.DMA((2, GROUP, 2)),
            pltpu.SemaphoreType.DMA((GROUP, 2)),
            pltpu.SemaphoreType.DMA((n_bits, n_sub, R1 + 1)),
            pltpu.SemaphoreType.DMA((n_sub, R1 + 1)),
            pltpu.SemaphoreType.DMA((4,)),
        ],
        compiler_params=pltpu.CompilerParams(
            collective_id=0, has_side_effects=True, vmem_limit_bytes=56 * 1024 * 1024
        ),
    )(q_heads.T, k_heads.T, v_heads.T, w_out, offsets, valid).T


def solution(mesh):
    spread = P(("slides", "seq"), "sub")
    return jax.shard_map(
        functools.partial(local, mesh.shape["seq"], mesh.shape["sub"]),
        mesh=mesh,
        in_specs=(spread, spread, spread, P(), P(), P("slides")),
        out_specs=spread,
        check_vma=False,
    )
```

time: 37 us -> 34.6 us (0.935)
  Pallas kernels: 34.4 us -> 31.9 us
    pallas_call x1, Pallas kernels: 34.4 us -> 31.9 us  [local(): pl.pallas_call(functools.partial(kernel, n_seq, n_sub, heads), out_shape=...]
where the time goes in v3:
time: 34.6 us; the launch traced here: 34.4 us
  Pallas kernels  31.9 us (92%)
  local copies, waits for them, and re-layouts  1.77 us (5%)
  between operations  0.66 us (2%)
    pallas_call x1, Pallas kernels, local(): pl.pallas_call(functools.partial(kernel, n_seq, n_sub, heads), out_shape=...  31.9 us
    unnamed x1, local copies, waits for them, and re-layouts  1.77 us

profile of v3, /device:TPU:1, one launch (start us, length us, event | category | flops | bytes accessed | tf_op | source)
XLA Modules:
  0.0 34.4 jit_solution(17596649658536940630)
XLA Ops:
  0.7 31.9 %shard_map.64 = bf16[192,1024]{1,0:T(8,128)(2,1)} custom-call(bf16[192,1024]{1,0:T(8,128)(2,1)} %bitcast.5, bf16[192,1024]{1,0:T(8,128)(2,1)} %bitcast.6, bf16[192,1024]{1,0:T(8,128)(2,1)} %bitcast.7, bf16[768,768]{1,0:T(8,128)(2,1)} %w_hbm.1, s32[2,16]{1,0:T(2,128)} %off_ref.1, s32[1]{0:T(128)S(6)} %copy.8.valid_ref), custom_call_target="tpu_custom_call" | custom-call | tf_op jit(solution)/shard_map/pallas_call | solution.py:520
  32.6 1.8 %copy.9 = bf16[1024,192]{0,1:T(8,128)(2,1)} copy(bf16[1024,192]{0,1:T(8,128)(2,1)} %bitcast.4) | data formatting | bytes 786432

commit v4 on v3

--- a/solution.py
+++ b/solution.py
@@ -481,8 +481,7 @@
                 axis=0,
             )
             res = lax.dot_general(picked, one_hot, contract_first, preferred_element_type=jnp.float32)
-            place = block0 + blk * square + lax.broadcasted_iota(jnp.int32, (1, square), 1)
-            o_ref[:, pl.ds(blk * square, square)] = jnp.where(place < limit, res, 0.0).astype(jnp.bfloat16)
+            o_ref[:, pl.ds(blk * square, square)] = res.astype(jnp.bfloat16)
 
     with jax.named_scope("drain"):
         for o in range(n_seq):
@@ -517,7 +516,7 @@
     vmem = pl.BlockSpec(memory_space=pltpu.VMEM)
     smem = pl.BlockSpec(memory_space=pltpu.SMEM)
     wide_all = n_seq * strip
-    return pl.pallas_call(
+    out = pl.pallas_call(
         functools.partial(kernel, n_seq, n_sub, heads),
         out_shape=jax.ShapeDtypeStruct((cols, rows), bf),
         in_specs=[pl.BlockSpec(memory_space=pl.ANY)] * 4 + [smem] * 2,
@@ -555,9 +554,11 @@
             pltpu.SemaphoreType.DMA((4,)),
         ],
         compiler_params=pltpu.CompilerParams(
-            collective_id=0, has_side_effects=True, vmem_limit_bytes=56 * 1024 * 1024
+            collective_id=0, has_side_effects=True, vmem_limit_bytes=32 * 1024 * 1024
         ),
-    )(q_heads.T, k_heads.T, v_heads.T, w_out, offsets, valid).T
+    )(q_heads.T, k_heads.T, v_heads.T, w_out, offsets, valid)
+    place = lax.axis_index("seq") * rows + lax.broadcasted_iota(jnp.int32, (1, rows), 1)
+    return jnp.where(place < valid[0], out, jnp.zeros((), bf)).T
 
 
 def solution(mesh):

time: 34.6 us -> 38 us (1.098)
  local copies, waits for them, and re-layouts: 1.77 us -> 4.93 us
  other arithmetic: 0 us -> 0.78 us
  Pallas kernels: 31.9 us -> 31.4 us
    unnamed x1 -> x10, local copies, waits for them, and re-layouts: 1.77 us -> 4.93 us
    transpose x0 -> x1, other arithmetic: none -> 0.78 us  [local(): return jnp.where(place < valid[0], out, jnp.zeros((), bf)).T]
    pallas_call x1, Pallas kernels: 31.9 us -> 31.4 us  [local(): pl.pallas_call(functools.partial(kernel, n_seq, n_sub, heads), out_shape=...]
where the time goes in v4:
time: 38 us; the launch traced here: 37.8 us
  Pallas kernels  31.4 us (83%)
  local copies, waits for them, and re-layouts  4.93 us (13%)
  other arithmetic  0.78 us (2%)
  between operations  0.68 us (2%)
    pallas_call x1, Pallas kernels, local(): pl.pallas_call(functools.partial(kernel, n_seq, n_sub, heads), out_shape=...  31.4 us
    unnamed x10, local copies, waits for them, and re-layouts  4.93 us
    transpose x1, other arithmetic, local(): return jnp.where(place < valid[0], out, jnp.zeros((), bf)).T  0.78 us

profile of v4, /device:TPU:1, one launch (start us, length us, event | category | flops | bytes accessed | tf_op | source)
XLA Modules:
  0.0 37.8 jit_solution(3308332983322358128)
XLA Ops:
  0.7 0.0 copy-start
  0.7 1.3 %copy-done = bf16[768,768]{1,0:T(8,128)(2,1)S(1)} copy-done((bf16[768,768]{1,0:T(8,128)(2,1)S(1)}, bf16[768,768]{1,0:T(8,128)(2,1)}, u32[]{:S(2)}) %copy-start) | copy-done | bytes 1179672
  1.9 0.0 copy-start.1
  1.9 1.0 %copy-done.1 = bf16[1024,192]{0,1:T(8,128)(2,1)S(1)} copy-done((bf16[1024,192]{0,1:T(8,128)(2,1)S(1)}, bf16[1024,192]{0,1:T(8,128)(2,1)}, u32[]{:S(2)}) %copy-start.1) | copy-done | bytes 393240
  2.9 0.0 copy-start.2
  2.9 1.0 %copy-done.2 = bf16[1024,192]{0,1:T(8,128)(2,1)S(1)} copy-done((bf16[1024,192]{0,1:T(8,128)(2,1)S(1)}, bf16[1024,192]{0,1:T(8,128)(2,1)}, u32[]{:S(2)}) %copy-start.2) | copy-done | bytes 393240
  3.9 0.0 copy-start.3
  3.9 1.0 %copy-done.3 = bf16[1024,192]{0,1:T(8,128)(2,1)S(1)} copy-done((bf16[1024,192]{0,1:T(8,128)(2,1)S(1)}, bf16[1024,192]{0,1:T(8,128)(2,1)}, u32[]{:S(2)}) %copy-start.3) | copy-done | bytes 393240
  4.9 0.0 copy-start.4
  4.9 0.7 %copy-done.4 = s32[2,16]{1,0:T(2,128)S(1)} copy-done((s32[2,16]{1,0:T(2,128)S(1)}, s32[2,16]{1,0:T(2,128)}, u32[]{:S(2)}) %copy-start.4) | copy-done | bytes 152
  5.6 31.4 %shard_map.64 = bf16[192,1024]{1,0:T(8,128)(2,1)S(1)} custom-call(bf16[192,1024]{1,0:T(8,128)(2,1)S(1)} %bitcast.7, bf16[192,1024]{1,0:T(8,128)(2,1)S(1)} %bitcast.8, bf16[192,1024]{1,0:T(8,128)(2,1)S(1)} %bitcast.9, bf16[768,768]{1,0:T(8,128)(2,1)S(1)} %copy-done, s32[2,16]{1,0:T(2,128)S(1)} %copy-done.4, s32[1]{0:T(128)} %copy.7.valid_ref), custom_call_target="tpu_custom_call" | custom-call | tf_op jit(solution)/shard_map/pallas_call | solution.py:519
  37.0 0.8 %select_bitcast_fusion = bf16[1024,192]{0,1:T(8,128)(2,1)} fusion(bf16[192,1024]{1,0:T(8,128)(2,1)S(1)} %shard_map.64, pred[1024]{0:T(1024)(128)(4,1)S(1)} %add_compare_fusion), kind=kLoop, calls=%fused_computation | loop fusion | flops 196608 | bytes 787456 | tf_op jit(solution)/shard_map/transpose | solution.py:561
  (1 shorter events, 0.0 us)
Async XLA Ops:
  0.7 1.3 %copy-start = (bf16[768,768]{1,0:T(8,128)(2,1)S(1)}, bf16[768,768]{1,0:T(8,128)(2,1)}, u32[]{:S(2)}) copy-start(bf16[768,768]{1,0:T(8,128)(2,1)} %w_hbm.1) | copy-start | bytes 3538948
  1.9 1.0 %copy-start.1 = (bf16[1024,192]{0,1:T(8,128)(2,1)S(1)}, bf16[1024,192]{0,1:T(8,128)(2,1)}, u32[]{:S(2)}) copy-start(bf16[1024,192]{0,1:T(8,128)(2,1)} %param.6) | copy-start | bytes 1179652
  2.9 1.0 %copy-start.2 = (bf16[1024,192]{0,1:T(8,128)(2,1)S(1)}, bf16[1024,192]{0,1:T(8,128)(2,1)}, u32[]{:S(2)}) copy-start(bf16[1024,192]{0,1:T(8,128)(2,1)} %param.7) | copy-start | bytes 1179652
  3.9 1.0 %copy-start.3 = (bf16[1024,192]{0,1:T(8,128)(2,1)S(1)}, bf16[1024,192]{0,1:T(8,128)(2,1)}, u32[]{:S(2)}) copy-start(bf16[1024,192]{0,1:T(8,128)(2,1)} %param.8) | copy-start | bytes 1179652
  4.9 0.7 %copy-start.4 = (s32[2,16]{1,0:T(2,128)S(1)}, s32[2,16]{1,0:T(2,128)}, u32[]{:S(2)}) copy-start(s32[2,16]{1,0:T(2,128)} %off_ref.1) | copy-start | bytes 388
